TPU v7x, 8 devices: a whole 2x2x1 slice. The times are simulated.
8 devices in a mesh: pair: 1 (over z), tp: 2 (over y), side: 4 (over x, core).
Axes of the slice: x: 2, y: 2, z: 1, core: 2. Of those that a mesh axis runs over, the one named last changes fastest.
Arguments:
- x: bfloat16 [2048, 4096], P(('pair', 'side'))
- req_len: int32 [4], P('pair')
- dest: int32 [4], P('pair')
- w_qkv: bfloat16 [2, 4096, 12288], replicated
- w_out: bfloat16 [2, 4096, 4096], replicated
- w_gate: bfloat16 [2, 4096, 11008], replicated
- w_up: bfloat16 [2, 4096, 11008], replicated
- w_down: bfloat16 [2, 11008, 4096], replicated
- y_tok: bfloat16 [4, 32, 4096], P(('pair', 'side'))
- k_cache: bfloat16 [4, 2, 32, 64, 32, 128], P(('pair', 'side'), None, None, None, 'tp')
- v_cache: bfloat16 [4, 2, 32, 64, 32, 128], P(('pair', 'side'), None, None, None, 'tp')
- c_len: int32 [4, 32], P(('pair', 'side'))
Outputs:
- output 1: bfloat16 [2048, 4096], P(('pair', 'side'))
- output 2: bfloat16 [4, 32, 4096], P(('pair', 'side'))
- output 3: bfloat16 [4, 2, 896, 32, 128], P(('pair', 'side'), None, None, 'tp')
- output 4: bfloat16 [4, 2, 896, 32, 128], P(('pair', 'side'), None, None, 'tp')
- output 5: bfloat16 [4, 2, 32, 64, 32, 128], P(('pair', 'side'), None, None, None, 'tp')
- output 6: bfloat16 [4, 2, 32, 64, 32, 128], P(('pair', 'side'), None, None, None, 'tp')
All inputs are finite; a program needn't handle non-finite values.
Results may differ from a plain program's by a relative error of at most 0.0168853.
Values are sent between devices in bfloat16 or wider.
A program may use at most 3.5 GiB of HBM per device.

v0:
```python
import jax
import jax.numpy as jnp
from jax import lax
from jax.sharding import PartitionSpec as P

ROPE_BASE = 10000.0
NORM_EPS = 1e-5


def rms_norm(hidden):
    wide_vals = hidden.astype(jnp.float32)
    norm_scale = lax.rsqrt(jnp.mean(wide_vals * wide_vals, axis=-1, keepdims=True) + NORM_EPS)
    return (wide_vals * norm_scale).astype(jnp.bfloat16)


def rotary(vectors, positions):
    half_dim = vectors.shape[-1] // 2
    inv_freq = ROPE_BASE ** (-jnp.arange(half_dim, dtype=jnp.float32) / half_dim)
    angles = positions.astype(jnp.float32)[:, None, None] * inv_freq
    cos_val = jnp.cos(angles)
    sin_val = jnp.sin(angles)
    wide_vals = vectors.astype(jnp.float32)
    lead_half = wide_vals[..., :half_dim]
    tail_half = wide_vals[..., half_dim:]
    return jnp.concatenate([lead_half * cos_val - tail_half * sin_val, tail_half * cos_val + lead_half * sin_val], axis=-1).astype(jnp.bfloat16)


def head_columns(block, groups, tp_size, tp_idx, interleaved):
    row_count, col_count = block.shape
    group_width = col_count // groups
    local_groups = groups // tp_size
    if interleaved:
        head_view = block.reshape(row_count, local_groups, tp_size, group_width)
        return lax.dynamic_index_in_dim(head_view, tp_idx, axis=2, keepdims=False).reshape(row_count, local_groups * group_width)
    return lax.dynamic_slice_in_dim(block, tp_idx * local_groups * group_width, local_groups * group_width, axis=1)


def head_rows(block, groups, tp_size, tp_idx, interleaved):
    row_count, col_count = block.shape
    group_height = row_count // groups
    local_groups = groups // tp_size
    if interleaved:
        head_view = block.reshape(local_groups, tp_size, group_height, col_count)
        return lax.dynamic_index_in_dim(head_view, tp_idx, axis=1, keepdims=False).reshape(local_groups * group_height, col_count)
    return lax.dynamic_slice_in_dim(block, tp_idx * local_groups * group_height, local_groups * group_height, axis=0)


def layer_weights(w_qkv, w_out, w_gate, w_up, w_down, layer, kv_heads, tp_size, tp_idx, interleaved):
    q_cols = w_out.shape[1]
    kv_cols = (w_qkv.shape[2] - q_cols) // 2
    qkv_l = w_qkv[layer]
    wq_l = head_columns(qkv_l[:, :q_cols], kv_heads, tp_size, tp_idx, interleaved)
    wk_l = head_columns(qkv_l[:, q_cols:q_cols + kv_cols], kv_heads, tp_size, tp_idx, interleaved)
    wv_l = head_columns(qkv_l[:, q_cols + kv_cols:], kv_heads, tp_size, tp_idx, interleaved)
    wo_l = head_rows(w_out[layer], kv_heads, tp_size, tp_idx, interleaved)
    ff_local = w_gate.shape[2] // tp_size
    wg_l = lax.dynamic_slice_in_dim(w_gate[layer], tp_idx * ff_local, ff_local, axis=1)
    wu_l = lax.dynamic_slice_in_dim(w_up[layer], tp_idx * ff_local, ff_local, axis=1)
    wd_l = lax.dynamic_slice_in_dim(w_down[layer], tp_idx * ff_local, ff_local, axis=0)
    return wq_l, wk_l, wv_l, wo_l, wg_l, wu_l, wd_l


def project(hidden, wq_l, wk_l, wv_l, positions, kv_local, group_rep):
    row_count = hidden.shape[0]
    head_dim = wk_l.shape[1] // kv_local
    normed = rms_norm(hidden)
    query = jnp.dot(normed, wq_l, preferred_element_type=jnp.float32).astype(jnp.bfloat16)
    key_new = jnp.dot(normed, wk_l, preferred_element_type=jnp.float32).astype(jnp.bfloat16)
    value_new = jnp.dot(normed, wv_l, preferred_element_type=jnp.float32).astype(jnp.bfloat16)
    query = rotary(query.reshape(row_count, kv_local * group_rep, head_dim), positions)
    key_new = rotary(key_new.reshape(row_count, kv_local, head_dim), positions)
    return query.reshape(row_count, kv_local, group_rep, head_dim), key_new, value_new.reshape(row_count, kv_local, head_dim)


def finish_layer(hidden, context, wo_l, wg_l, wu_l, wd_l):
    attn_out = lax.psum(jnp.dot(context, wo_l, preferred_element_type=jnp.float32), 'tp').astype(jnp.bfloat16)
    hidden = (hidden.astype(jnp.float32) + attn_out.astype(jnp.float32)).astype(jnp.bfloat16)
    normed = rms_norm(hidden)
    gate = jnp.dot(normed, wg_l, preferred_element_type=jnp.float32).astype(jnp.bfloat16)
    upper = jnp.dot(normed, wu_l, preferred_element_type=jnp.float32).astype(jnp.bfloat16)
    activated = (jax.nn.silu(gate.astype(jnp.float32)) * upper.astype(jnp.float32)).astype(jnp.bfloat16)
    down = lax.psum(jnp.dot(activated, wd_l, preferred_element_type=jnp.float32), 'tp').astype(jnp.bfloat16)
    return (hidden.astype(jnp.float32) + down.astype(jnp.float32)).astype(jnp.bfloat16)


def prompt_attention(query, key_new, value_new, allowed):
    score_scale = query.shape[-1] ** -0.5
    scores = jnp.einsum('sjrd,tjd->jrst', query, key_new, preferred_element_type=jnp.float32) * score_scale
    scores = jnp.where(allowed, scores, -1e30)
    attn_prob = jax.nn.softmax(scores, axis=-1).astype(jnp.bfloat16)
    context = jnp.einsum('jrst,tjd->sjrd', attn_prob, value_new, preferred_element_type=jnp.float32).astype(jnp.bfloat16)
    return context.reshape(query.shape[0], -1)


def decode_attention(query, k_layer, v_layer, lengths):
    score_scale = query.shape[-1] ** -0.5
    cache_pos = jnp.arange(k_layer.shape[1])
    visible = cache_pos[None, :] <= lengths[:, None]
    scores = jnp.einsum('bjrd,btjd->bjrt', query, k_layer, preferred_element_type=jnp.float32) * score_scale
    scores = jnp.where(visible[:, None, None, :], scores, -1e30)
    attn_prob = jax.nn.softmax(scores, axis=-1).astype(jnp.bfloat16)
    context = jnp.einsum('bjrt,btjd->bjrd', attn_prob, v_layer, preferred_element_type=jnp.float32).astype(jnp.bfloat16)
    return context.reshape(query.shape[0], -1)


def write_slot(cache, row_new, lengths):
    return jax.vmap(lambda one_cache, one_row, one_len: lax.dynamic_update_slice_in_dim(one_cache, one_row[None], one_len, axis=0))(cache, row_new, lengths)


def segments(req_len, seq_len):
    row_ids = jnp.arange(seq_len)
    past_end = row_ids[:, None] >= jnp.cumsum(req_len)[None, :]
    seg_id = jnp.sum(past_end.astype(jnp.int32), axis=1)
    positions = row_ids - jnp.sum(jnp.where(past_end, req_len[None, :], 0), axis=1)
    allowed = (seg_id[:, None] == seg_id[None, :]) & (row_ids[None, :] <= row_ids[:, None])
    return positions, allowed


def pick_interleaved(full, tp_size, tp_idx):
    shape_in = full.shape
    head_view = full.reshape(shape_in[:2] + (shape_in[2] // tp_size, tp_size) + shape_in[3:])
    return lax.dynamic_index_in_dim(head_view, tp_idx, axis=3, keepdims=False)


def request_pieces(full, req_len, dest, max_req):
    side_size = req_len.shape[0]
    starts = jnp.cumsum(req_len) - req_len
    match = dest[None, :] == jnp.arange(side_size)[:, None]
    start_of = jnp.sum(jnp.where(match, starts[None, :], 0), axis=1)
    length_of = jnp.sum(jnp.where(match, req_len[None, :], 0), axis=1)
    padded = jnp.concatenate([full, jnp.zeros((full.shape[0], max_req) + full.shape[2:], full.dtype)], axis=1)

    def one_group(start_row, length):
        piece = lax.dynamic_slice_in_dim(padded, start_row, max_req, axis=1)
        keep = (jnp.arange(max_req) < length)[None, :, None, None]
        return jnp.where(keep, piece, jnp.zeros_like(piece))

    return jax.vmap(one_group)(start_of, length_of)


def solution(mesh):
    tp_size = mesh.shape['tp']
    side_size = mesh.shape['side']
    rows_spec = P(('pair', 'side'), None)
    batch_spec = P(('pair', 'side'), None, None)
    cache_spec = P(('pair', 'side'), None, None, None, 'tp', None)
    prompt_spec = P(('pair', 'side'), None, None, 'tp', None)

    def local_step(x_loc, req_len, dest, w_qkv, w_out, w_gate, w_up, w_down, y_loc, kc_loc, vc_loc, clen_loc):
        side_idx = lax.axis_index('side')
        tp_idx = lax.axis_index('tp')
        layers = w_qkv.shape[0]
        head_dim = kc_loc.shape[-1]
        kv_local = kc_loc.shape[-2]
        kv_heads = kv_local * tp_size
        group_rep = w_out.shape[1] // head_dim // kv_heads
        prompt_rows, model_dim = x_loc.shape
        seq_len = prompt_rows * side_size
        max_req = 2 * prompt_rows - prompt_rows // 4

        x_full = lax.all_gather(x_loc, 'side', axis=0, tiled=True)
        positions, allowed = segments(req_len, seq_len)

        def run_prefill(x_rows):
            hidden = x_rows
            keys_all = []
            values_all = []
            for layer in range(layers):
                wq_l, wk_l, wv_l, wo_l, wg_l, wu_l, wd_l = layer_weights(w_qkv, w_out, w_gate, w_up, w_down, layer, kv_heads, tp_size, tp_idx, False)
                query, key_new, value_new = project(hidden, wq_l, wk_l, wv_l, positions, kv_local, group_rep)
                keys_all.append(key_new)
                values_all.append(value_new)
                context = prompt_attention(query, key_new, value_new, allowed)
                hidden = finish_layer(hidden, context, wo_l, wg_l, wu_l, wd_l)
            return hidden, jnp.stack(keys_all), jnp.stack(values_all)

        def skip_prefill(x_rows):
            kv_shape = (layers, seq_len, kv_local, head_dim)
            return jnp.zeros_like(x_rows), jnp.zeros(kv_shape, jnp.bfloat16), jnp.zeros(kv_shape, jnp.bfloat16)

        hidden, keys_loc, values_loc = lax.cond(side_idx == 0, run_prefill, skip_prefill, x_full)
        keys_full = lax.all_gather(keys_loc, 'tp', axis=2, tiled=True)
        values_full = lax.all_gather(values_loc, 'tp', axis=2, tiled=True)
        k_send = request_pieces(pick_interleaved(keys_full, tp_size, tp_idx), req_len, dest, max_req)
        v_send = request_pieces(pick_interleaved(values_full, tp_size, tp_idx), req_len, dest, max_req)
        k_recv = lax.all_to_all(k_send, 'side', 0, 0, tiled=True)[0]
        v_recv = lax.all_to_all(v_send, 'side', 0, 0, tiled=True)[0]
        hidden_rows = lax.all_to_all(hidden.reshape(side_size, prompt_rows, model_dim), 'side', 0, 0, tiled=True)[0]

        lengths = clen_loc[0]
        hidden_dec = y_loc[0]
        k_out = []
        v_out = []
        for layer in range(layers):
            wq_l, wk_l, wv_l, wo_l, wg_l, wu_l, wd_l = layer_weights(w_qkv, w_out, w_gate, w_up, w_down, layer, kv_heads, tp_size, tp_idx, True)
            query, key_new, value_new = project(hidden_dec, wq_l, wk_l, wv_l, lengths, kv_local, group_rep)
            k_layer = write_slot(kc_loc[0, layer], key_new, lengths)
            v_layer = write_slot(vc_loc[0, layer], value_new, lengths)
            context = decode_attention(query, k_layer, v_layer, lengths)
            hidden_dec = finish_layer(hidden_dec, context, wo_l, wg_l, wu_l, wd_l)
            k_out.append(k_layer)
            v_out.append(v_layer)
        return hidden_rows, hidden_dec[None], k_recv[None], v_recv[None], jnp.stack(k_out)[None], jnp.stack(v_out)[None]

    return jax.shard_map(local_step, mesh=mesh,
                         in_specs=(rows_spec, P('pair'), P('pair'), P(), P(), P(), P(), P(), batch_spec, cache_spec, cache_spec, rows_spec),
                         out_specs=(rows_spec, batch_spec, prompt_spec, prompt_spec, cache_spec, cache_spec),
                         check_vma=False)
```

profile of v0, /device:TPU:0, one launch (start us, length us, event | category | flops | bytes accessed | tf_op | source)
XLA Modules:
  0.0 6956.2 jit_solution(12655909174404528590)
XLA Ops:
  7.9 130.2 %fusion.341 = (bf16[1,4096,12288]{2,1,0:T(8,128)(2,1)}, bf16[1,4096,12288]{2,1,0:T(8,128)(2,1)}) fusion(bf16[2,4096,12288]{2,1,0:T(8,128)(2,1)} %param.17), kind=kLoop, calls=%fused_computation.382 | loop fusion | bytes 402653184 | tf_op jit(solution)/shard_map/slice | solution.py:51
  138.1 115.2 %copy.124 = bf16[1,4096,12288]{1,2,0:T(8,128)(2,1)} copy(bf16[1,4096,12288]{2,1,0:T(8,128)(2,1)} %get-tuple-element.288) | data formatting | bytes 201326592
  253.3 64.7 fusion.346
  318.2 23.3 constant_dynamic-slice_fusion.10
  416.8 227.9 %while.8 = (s32[]{:T(128)}, bf16[32,64,16,128]{3,2,1,0:T(8,128)(2,1)}, s32[32,4]{0,1:T(4,128)S(1)}, bf16[32,1,16,128]{3,2,1,0:T(8,128)(2,1)S(1)}, s32[]{:T(128)}, /*index=5*/s32[4]{0:T(128)S(1)}) while((s32[]{:T(128)}, bf16[32,64,16,128]{3,2,1,0:T(8,128)(2,1)}, s32[32,4]{0,1:T(4,128)S(1)}, bf16[32,1,16,128]{3,2,1,0:T(8,128)(2,1)S(1)}, s32[]{:T(128)}, ...), condition=%wide.while_cond.2, body=%wide.while_body.2.sunk | while | flops 2077 | bytes 14506 | solution.py:107
  660.8 4340.3 %conditional.1 = (bf16[2048,4096]{1,0:T(8,128)(2,1)}, bf16[2,2048,16,128]{3,1,2,0:T(8,128)(2,1)}, bf16[2,2048,16,128]{1,3,2,0:T(8,128)(2,1)}) conditional(s32[]{:T(128)} %convert_element_type.391, () %tuple.16, (bf16[2048,4096]{1,0:T(8,128)(2,1)}, bf16[2,4096,12288]{2,1,0:T(8,128)(2,1)}, s32[]{:T(128)}, s32[2048,4]{0,1:T(4,128)}, s32[2048]{0:T(1024)}, ...), branch_computations={%region_3.4_spmd, %region_4.17_spmd} | conditional | flops 900260298752 | bytes 5652726272 | solution.py:181
  669.0 130.1 %slice_bitcast_fusion.1 = (bf16[4096,12288]{1,0:T(8,128)(2,1)}, bf16[4096,12288]{1,0:T(8,128)(2,1)}) fusion(bf16[2,4096,12288]{2,1,0:T(8,128)(2,1)} %get-tuple-element.19), kind=kLoop, calls=%fused_computation.15 | loop fusion | bytes 402653184 | tf_op jit(solution)/shard_map/cond/branch_1_fun/squeeze | solution.py:51
  799.1 64.7 fusion.335
  863.8 62.7 fusion.99
  962.4 62.9 fusion.102
  1065.3 35.3 subtract_convert_fusion.2
  1114.4 105.8 %fusion.2 = (f32[16,2048]{1,0:T(8,128)S(1)}, f32[16,2048,2048]{2,1,0:T(8,128)}) fusion(pred[2048,2048]{0,1:T(8,128)(4,1)} %compare_and_fusion, bf16[2048,16,64]{2,0,1:T(8,128)(2,1)} %get-tuple-element.265, bf16[2048,16,64]{2,0,1:T(8,128)(2,1)} %get-tuple-element.264, bf16[2048,16,64]{2,0,1:T(8,128)(2,1)} %get-tuple-element.278, ...), kind=kOutput, calls=%fused_computation.8 | convolution fusion | flops 17414717440 | bytes 289538048 | tf_op jit(solution)/shard_map/cond/branch_1_fun/sjrd,tjd->jrst/dot_general | solution.py:88
  1220.2 81.8 %fusion = f32[16,2048]{1,0:T(8,128)S(1)} fusion(f32[16,2048,2048]{2,1,0:T(8,128)} %get-tuple-element.283, f32[16,2048]{1,0:T(8,128)S(1)} %get-tuple-element.282, pred[2048,2048]{0,1:T(8,128)(4,1)} %compare_and_fusion), kind=kLoop, calls=%fused_computation.6 | loop fusion | flops 268402688 | bytes 272891904 | tf_op jit(solution)/shard_map/cond/branch_1_fun/reduce_sum | solution.py:90
  1302.0 63.1 fusion.96
  1365.2 95.0 %fusion.118 = bf16[16,128,2048]{2,1,0:T(8,128)(2,1)} fusion(bf16[2048,16,128]{0,2,1:T(8,128)(2,1)} %bitcast.434, f32[16,2048]{1,0:T(8,128)S(1)} %fusion, f32[16,2048]{1,0:T(8,128)S(1)} %get-tuple-element.282, f32[16,2048,2048]{2,1,0:T(8,128)} %get-tuple-element.283, pred[2048,2048]{0,1:T(8,128)(4,1)} %compare_and_fusion), kind=kOutput, calls=%fused_computation.125 | convolution fusion | flops 17519607808 | bytes 289669120 | tf_op jit(solution)/shard_map/cond/branch_1_fun/jrst,tjd->sjrd/dot_general | solution.py:91
  1460.2 43.5 fusion.336
  1503.7 43.9 fusion.66
  1547.6 409.7 %all-reduce.11 = bf16[2048,4096]{1,0:T(8,128)(2,1)} all-reduce(f32[2048,4096]{1,0:T(8,128)} %fusion.66), channel_id=1, replica_groups=mesh['pair'=1,'tp'=2,'side'=4] {'tp'}, use_global_device_ids=true, to_apply=%region_8.8 | all-reduce | flops 8388608 | bytes 50331648 | tf_op jit(solution)/shard_map/cond/branch_1_fun/psum | solution.py:76
  1957.4 19.9 fusion.39
  1977.9 232.4 %fusion.332 = (bf16[1,4096,11008]{2,1,0:T(8,128)(2,1)}, bf16[1,4096,11008]{2,1,0:T(8,128)(2,1)}, bf16[1,4096,11008]{2,1,0:T(8,128)(2,1)}, bf16[1,4096,11008]{2,1,0:T(8,128)(2,1)}) fusion(bf16[2,4096,11008]{2,1,0:T(8,128)(2,1)} %get-tuple-element.24, bf16[2,4096,11008]{2,1,0:T(8,128)(2,1)} %get-tuple-element.25), kind=kLoop, calls=%fused_computation.373 | loop fusion | bytes 721420288 | tf_op jit(solution)/shard_map/cond/branch_1_fun/slice | solution.py:57
  2210.3 111.1 %fusion.53 = bf16[2048,5504]{1,0:T(8,128)(2,1)} fusion(bf16[1,4096,11008]{2,1,0:T(8,128)(2,1)} %get-tuple-element.286, s32[]{:T(128)S(6)} %select_n.88, bf16[2048,4096]{1,0:T(8,128)(2,1)} %get-tuple-element.221, f32[2048]{0:T(1024)S(1)} %copy-done.35), kind=kOutput, calls=%fused_computation.73 | convolution fusion | flops 92378234880 | bytes 84418560 | tf_op jit(solution)/shard_map/cond/branch_1_fun/dot_general | solution.py:80
  2321.4 119.1 %fusion.35 = bf16[2048,5504]{1,0:T(8,128)(2,1)} fusion(bf16[2048,5504]{1,0:T(8,128)(2,1)} %fusion.53, bf16[1,4096,11008]{2,1,0:T(8,128)(2,1)} %get-tuple-element.249, s32[]{:T(128)S(6)} %select_n.88, bf16[2048,4096]{1,0:T(8,128)(2,1)} %get-tuple-element.221, f32[2048]{0:T(1024)S(1)} %copy-done.35), kind=kOutput, calls=%fused_computation.59 | convolution fusion | flops 92468412416 | bytes 106962944 | tf_op jit(solution)/shard_map/cond/branch_1_fun/dot_general | solution.py:79
  2440.5 116.3 %fusion.331 = (bf16[1,11008,4096]{2,1,0:T(8,128)(2,1)}, bf16[1,11008,4096]{2,1,0:T(8,128)(2,1)}) fusion(bf16[2,11008,4096]{2,1,0:T(8,128)(2,1)} %get-tuple-element.26), kind=kLoop, calls=%fused_computation.372 | loop fusion | bytes 360710144 | tf_op jit(solution)/shard_map/cond/branch_1_fun/slice | solution.py:59
  2556.8 108.6 %fusion.22 = f32[2048,4096]{1,0:T(8,128)} fusion(bf16[2048,5504]{1,0:T(8,128)(2,1)} %fusion.35, bf16[1,11008,4096]{2,1,0:T(8,128)(2,1)} %get-tuple-element.247, s32[]{:T(128)S(6)} %select_n.88), kind=kOutput, calls=%fused_computation.46 | convolution fusion | flops 92341796864 | bytes 101187584 | tf_op jit(solution)/shard_map/cond/branch_1_fun/dot_general | solution.py:82
  2665.4 406.3 %all-reduce.12 = bf16[2048,4096]{1,0:T(8,128)(2,1)} all-reduce(f32[2048,4096]{1,0:T(8,128)} %fusion.22), channel_id=1, replica_groups=mesh['pair'=1,'tp'=2,'side'=4] {'tp'}, use_global_device_ids=true, to_apply=%region_10.10 | all-reduce | flops 8388608 | bytes 50331648 | tf_op jit(solution)/shard_map/cond/branch_1_fun/psum | solution.py:82
  3071.7 19.9 fusion.42
  3091.6 64.7 fusion.334
  3156.3 62.7 fusion.108
  3254.8 63.1 fusion.111
  3353.8 34.5 subtract_convert_fusion
  3388.3 21.4 maximum_maximum_fusion
  3409.7 105.8 %fusion.3 = (f32[16,2048]{1,0:T(8,128)S(1)}, f32[16,2048,2048]{2,1,0:T(8,128)}) fusion(pred[2048,2048]{0,1:T(8,128)(4,1)} %compare_and_fusion, bf16[2048,16,64]{2,0,1:T(8,128)(2,1)} %get-tuple-element.261, bf16[2048,16,64]{2,0,1:T(8,128)(2,1)} %get-tuple-element.260, bf16[2048,16,64]{2,0,1:T(8,128)(2,1)} %get-tuple-element.276, ...), kind=kOutput, calls=%fused_computation.9 | convolution fusion | flops 17414717440 | bytes 289538048 | tf_op jit(solution)/shard_map/cond/branch_1_fun/sjrd,tjd->jrst/dot_general | solution.py:88
  3515.5 81.8 %fusion.1 = f32[16,2048]{1,0:T(8,128)S(1)} fusion(f32[16,2048,2048]{2,1,0:T(8,128)} %get-tuple-element.285, f32[16,2048]{1,0:T(8,128)S(1)} %get-tuple-element.284, pred[2048,2048]{0,1:T(8,128)(4,1)} %compare_and_fusion), kind=kLoop, calls=%fused_computation.7 | loop fusion | flops 268402688 | bytes 272891904 | tf_op jit(solution)/shard_map/cond/branch_1_fun/reduce_sum | solution.py:90
  3597.4 63.0 fusion.105
  3660.3 94.7 %fusion.121 = bf16[16,128,2048]{2,1,0:T(8,128)(2,1)} fusion(bf16[2048,16,128]{0,2,1:T(8,128)(2,1)} %bitcast.436, f32[16,2048]{1,0:T(8,128)S(1)} %fusion.1, f32[16,2048]{1,0:T(8,128)S(1)} %get-tuple-element.284, f32[16,2048,2048]{2,1,0:T(8,128)} %get-tuple-element.285, pred[2048,2048]{0,1:T(8,128)(4,1)} %compare_and_fusion), kind=kOutput, calls=%fused_computation.126 | convolution fusion | flops 17519607808 | bytes 289669120 | tf_op jit(solution)/shard_map/cond/branch_1_fun/jrst,tjd->sjrd/dot_general | solution.py:91
  3755.0 44.2 fusion.64
  3799.2 408.4 %all-reduce.13 = bf16[2048,4096]{1,0:T(8,128)(2,1)} all-reduce(f32[2048,4096]{1,0:T(8,128)} %fusion.64), channel_id=1, replica_groups=mesh['pair'=1,'tp'=2,'side'=4] {'tp'}, use_global_device_ids=true, to_apply=%region_14.14 | all-reduce | flops 8388608 | bytes 50331648 | tf_op jit(solution)/shard_map/cond/branch_1_fun/psum | solution.py:76
  4207.6 19.9 fusion.45
  4227.5 111.0 %fusion.61 = bf16[2048,5504]{1,0:T(8,128)(2,1)} fusion(bf16[1,4096,11008]{2,1,0:T(8,128)(2,1)} %get-tuple-element.287, s32[]{:T(128)S(6)} %select_n.88, bf16[2048,4096]{1,0:T(8,128)(2,1)} %get-tuple-element.217, f32[2048]{0:T(1024)S(1)} %add_rsqrt_fusion), kind=kOutput, calls=%fused_computation.75 | convolution fusion | flops 92378234880 | bytes 84418560 | tf_op jit(solution)/shard_map/cond/branch_1_fun/dot_general | solution.py:80
  4338.6 118.9 %fusion.34 = bf16[2048,5504]{1,0:T(8,128)(2,1)} fusion(bf16[2048,5504]{1,0:T(8,128)(2,1)} %fusion.61, bf16[1,4096,11008]{2,1,0:T(8,128)(2,1)} %get-tuple-element.248, s32[]{:T(128)S(6)} %select_n.88, bf16[2048,4096]{1,0:T(8,128)(2,1)} %get-tuple-element.217, f32[2048]{0:T(1024)S(1)} %add_rsqrt_fusion), kind=kOutput, calls=%fused_computation.58 | convolution fusion | flops 92468412416 | bytes 106962944 | tf_op jit(solution)/shard_map/cond/branch_1_fun/dot_general | solution.py:79
  4457.5 108.8 %fusion.16 = f32[2048,4096]{1,0:T(8,128)} fusion(bf16[2048,5504]{1,0:T(8,128)(2,1)} %fusion.34, bf16[1,11008,4096]{2,1,0:T(8,128)(2,1)} %get-tuple-element.246, s32[]{:T(128)S(6)} %select_n.88), kind=kOutput, calls=%fused_computation.40 | convolution fusion | flops 92341796864 | bytes 101187584 | tf_op jit(solution)/shard_map/cond/branch_1_fun/dot_general | solution.py:82
  4566.3 406.2 %all-reduce.14 = bf16[2048,4096]{1,0:T(8,128)(2,1)} all-reduce(f32[2048,4096]{1,0:T(8,128)} %fusion.16), channel_id=1, replica_groups=mesh['pair'=1,'tp'=2,'side'=4] {'tp'}, use_global_device_ids=true, to_apply=%region_16.16 | all-reduce | flops 8388608 | bytes 50331648 | tf_op jit(solution)/shard_map/cond/branch_1_fun/psum | solution.py:82
  4972.4 21.7 fusion.47
  5001.7 227.7 %while.9 = (s32[]{:T(128)}, bf16[32,64,16,128]{3,2,1,0:T(8,128)(2,1)}, s32[32,4]{0,1:T(4,128)S(1)}, bf16[32,1,16,128]{3,2,1,0:T(8,128)(2,1)}, s32[]{:T(128)}, /*index=5*/s32[4]{0:T(128)S(1)}) while((s32[]{:T(128)}, bf16[32,64,16,128]{3,2,1,0:T(8,128)(2,1)}, s32[32,4]{0,1:T(4,128)S(1)}, bf16[32,1,16,128]{3,2,1,0:T(8,128)(2,1)}, s32[]{:T(128)}, ...), condition=%wide.while_cond.3, body=%wide.while_body.3.sunk | while | flops 2077 | bytes 14506 | solution.py:107
  5243.4 43.5 fusion.347
  5294.3 115.2 %copy.126 = bf16[1,4096,12288]{1,2,0:T(8,128)(2,1)} copy(bf16[1,4096,12288]{2,1,0:T(8,128)(2,1)} %get-tuple-element.289) | data formatting | bytes 201326592
  5425.5 64.7 fusion.345
  5490.2 117.8 %fusion.342 = (bf16[1,4096,11008]{2,1,0:T(8,128)(2,1)}, bf16[1,4096,11008]{2,1,0:T(8,128)(2,1)}) fusion(bf16[2,4096,11008]{2,1,0:T(8,128)(2,1)} %param.19), kind=kLoop, calls=%fused_computation.383 | loop fusion | bytes 360710144 | tf_op jit(solution)/shard_map/slice | solution.py:57
  5608.1 118.0 %fusion.343 = (bf16[1,4096,11008]{2,1,0:T(8,128)(2,1)}, bf16[1,4096,11008]{2,1,0:T(8,128)(2,1)}) fusion(bf16[2,4096,11008]{2,1,0:T(8,128)(2,1)} %param.20), kind=kLoop, calls=%fused_computation.384 | loop fusion | bytes 360710144 | tf_op jit(solution)/shard_map/slice | solution.py:58
  5726.0 116.3 %fusion.344 = (bf16[1,11008,4096]{2,1,0:T(8,128)(2,1)}, bf16[1,11008,4096]{2,1,0:T(8,128)(2,1)}) fusion(bf16[2,11008,4096]{2,1,0:T(8,128)(2,1)} %param.21), kind=kLoop, calls=%fused_computation.385 | loop fusion | bytes 360710144 | tf_op jit(solution)/shard_map/slice | solution.py:59
  5876.2 46.6 copy.187
  5922.7 69.6 %all-gather.8.cloned.1.call-done = bf16[2,2048,32,128]{1,3,2,0:T(8,128)(2,1)} async-done(((bf16[2,2048,16,128]{1,3,2,0:T(8,128)(2,1)}), bf16[2,2048,32,128]{1,3,2,0:T(8,128)(2,1)}) %all-gather.8.cloned.1.call-update) | async-done | bytes 33554448 | tf_op jit(solution)/shard_map/all_gather | solution.py:183
  6006.5 23.6 copy.129
  6030.1 21.7 concatenate.115
  6051.9 28.9 concatenate.117
  6090.9 34.3 while.6
  6135.0 34.3 while.7
  6169.3 38.5 broadcast_select_fusion
  6217.2 31.7 fusion.164
  6266.6 23.5 constant_dynamic-slice_fusion.7
  6337.4 223.7 %while.10 = (s32[]{:T(128)}, bf16[32,64,16,128]{3,2,1,0:T(8,128)(2,1)}, s32[32,4]{0,1:T(4,128)S(1)}, bf16[32,1,16,128]{3,2,1,0:T(8,128)(2,1)S(1)}, s32[]{:T(128)}, /*index=5*/s32[4]{0:T(128)S(1)}) while((s32[]{:T(128)}, bf16[32,64,16,128]{3,2,1,0:T(8,128)(2,1)}, s32[32,4]{0,1:T(4,128)S(1)}, bf16[32,1,16,128]{3,2,1,0:T(8,128)(2,1)S(1)}, s32[]{:T(128)}, ...), condition=%wide.while_cond.4, body=%wide.while_body.4.sunk | while | flops 2077 | bytes 14506 | solution.py:107
  6578.4 227.5 %while.11 = (s32[]{:T(128)}, bf16[32,64,16,128]{3,2,1,0:T(8,128)(2,1)}, s32[32,4]{0,1:T(4,128)S(1)}, bf16[32,1,16,128]{3,2,1,0:T(8,128)(2,1)S(1)}, s32[]{:T(128)}, /*index=5*/s32[4]{0:T(128)S(1)}) while((s32[]{:T(128)}, bf16[32,64,16,128]{3,2,1,0:T(8,128)(2,1)}, s32[32,4]{0,1:T(4,128)S(1)}, bf16[32,1,16,128]{3,2,1,0:T(8,128)(2,1)S(1)}, s32[]{:T(128)}, ...), condition=%wide.while_cond.5, body=%wide.while_body.5.sunk | while | flops 2077 | bytes 14506 | solution.py:107
  6818.9 18.4 all-reduce.17
  6854.5 31.7 fusion.158
  (747 shorter events, 1534.4 us)
Async XLA Ops:
  7.2 637.5 %all-gather.4.cloned.1.call-start = ((), (), s32[]{:S(2)}) async-start(), calls=%async_computation.3 | async-start | bytes 20971520 | tf_op jit(solution)/shard_map/all_gather | solution.py:161
  7.9 5860.3 %all-gather.6.cloned.1.call-start = ((), (), s32[]{:S(2)}) async-start(), calls=%async_computation.4 | async-start | bytes 50331648 | tf_op jit(solution)/shard_map/all_gather | solution.py:182
  253.3 64.7 copy-start.9
  366.5 22.5 copy-start.38
  366.5 22.7 copy-start.42
  366.5 22.7 copy-start.46
  389.2 14.9 copy-start.47
  389.4 0.9 copy-start.22
  389.5 0.9 copy-start.24
  404.1 12.7 copy-start.18
  644.6 15.5 copy-start.13
  799.1 64.7 copy-start.31
  1048.9 12.5 copy-start.28
  1048.9 12.5 copy-start.40
  1048.9 12.6 copy-start.27
  1065.2 35.4 copy-start.3
  1065.2 35.3 copy-start.5
  1065.2 35.3 copy-start.26
  1220.2 81.8 %copy-start.32 = (f32[2048]{0:T(1024)S(1)}, f32[2048]{0:T(1024)}, u32[]{:S(2)}) copy-start(f32[2048]{0:T(1024)} %add_rsqrt_fusion.3) | copy-start | bytes 24580 | tf_op jit(solution)/shard_map/cond
  1977.9 232.4 %copy-start.35 = (f32[2048]{0:T(1024)S(1)}, f32[2048]{0:T(1024)}, u32[]{:S(2)}) copy-start(f32[2048]{0:T(1024)} %add_rsqrt_fusion.2) | copy-start | bytes 24580 | tf_op jit(solution)/shard_map/cond
  3091.6 163.2 %copy-start.33 = (f32[2048]{0:T(1024)}, f32[2048]{0:T(1024)S(1)}, u32[]{:S(2)}) copy-start(f32[2048]{0:T(1024)S(1)} %add_rsqrt_fusion.1) | copy-start | bytes 24580 | tf_op jit(solution)/shard_map/cond
  3341.4 12.4 copy-start.4
  3341.4 12.4 copy-start.6
  3515.5 81.8 %copy-start.34 = (f32[2048]{0:T(1024)S(1)}, f32[2048]{0:T(1024)}, u32[]{:S(2)}) copy-start(f32[2048]{0:T(1024)} %copy-done.33) | copy-start | bytes 24580 | tf_op jit(solution)/shard_map/cond
  4972.4 21.7 copy-start.7
  4972.4 21.7 copy-start.8
  5001.0 0.7 copy-start.14
  5001.0 0.7 copy-start.19
  5001.0 228.4 %copy-start.16 = (bf16[32,16,64]{2,1,0:T(8,128)(2,1)S(1)}, bf16[32,16,64]{2,1,0:T(8,128)(2,1)}, u32[]{:S(2)}) copy-start(bf16[32,16,64]{2,1,0:T(8,128)(2,1)} %get-tuple-element.312) | copy-start | bytes 196612
  5001.1 228.4 %copy-start.17 = (bf16[32,16,64]{2,1,0:T(8,128)(2,1)S(1)}, bf16[32,16,64]{2,1,0:T(8,128)(2,1)}, u32[]{:S(2)}) copy-start(bf16[32,16,64]{2,1,0:T(8,128)(2,1)} %get-tuple-element.313) | copy-start | bytes 196612
  5001.1 228.5 %copy-start.43 = (s32[1,32]{1,0:T(1,128)S(1)}, s32[1,32]{1,0:T(1,128)}, u32[]{:S(2)}) copy-start(s32[1,32]{1,0:T(1,128)} %param.25) | copy-start | bytes 388
  5001.1 991.2 %all-gather.8.cloned.1.call-start = ((), (), s32[]{:S(2)}) async-start(), calls=%async_computation.5 | async-start | bytes 50331648 | tf_op jit(solution)/shard_map/all_gather | solution.py:183
  5229.4 57.5 copy-start.20
  5229.6 57.3 copy-start.36
  5294.3 115.2 %copy-start.39 = (s32[4]{0:T(128)S(1)}, s32[4]{0:T(128)}, u32[]{:S(2)}) copy-start(s32[4]{0:T(128)} %param.15) | copy-start | bytes 52
  5294.3 115.2 %copy-start.48 = (s32[4,1]{0,1:T(1,128)S(1)}, s32[4,1]{0,1:T(1,128)}, u32[]{:S(2)}) copy-start(s32[4,1]{0,1:T(1,128)} %copy-done.47) | copy-start | bytes 52
  5294.3 115.2 %copy-start.44 = (s32[4]{0:T(128)S(1)}, s32[4]{0:T(128)}, u32[]{:S(2)}) copy-start(s32[4]{0:T(128)} %param.16) | copy-start | bytes 52
  5842.3 7.4 copy-start.45
  5842.3 7.6 copy-start.10
  5842.3 7.6 copy-start.12
  5842.3 7.9 copy-start.41
  5842.3 365.4 %all-to-all-start = ((bf16[4,512,4096]{2,1,0:T(8,128)(2,1)}), bf16[4,512,4096]{2,1,0:T(8,128)(2,1)}, u32[]{:S(2)}, u32[]{:S(2)}) async-start(bf16[4,512,4096]{2,1,0:T(8,128)(2,1)} %bitcast.40), calls=%async_computation | async-start | bytes 33554432 | tf_op jit(solution)/shard_map/all_to_all | solution.py:188
  5850.1 0.7 copy-start.1
  5850.1 0.7 copy-start.29
  6030.1 21.7 copy-start
  6207.8 9.4 copy-start.2
  6207.8 9.4 copy-start.11
  6207.8 9.4 copy-start.30
  6207.8 361.4 %all-to-all-start.1 = ((bf16[4,2,896,16,128]{4,3,2,1,0:T(8,128)(2,1)}), bf16[4,2,896,16,128]{4,3,2,1,0:T(8,128)(2,1)}, u32[]{:S(2)}, u32[]{:S(2)}) async-start(bf16[4,2,896,16,128]{4,3,2,1,0:T(8,128)(2,1)} %get-tuple-element.321), calls=%async_computation.1 | async-start | bytes 58720256 | tf_op jit(solution)/shard_map/all_to_all | solution.py:186
  6326.0 11.0 copy-start.23
  6326.0 11.0 copy-start.25
  6326.0 11.4 copy-start.15
  6326.0 11.4 copy-start.21
  6326.0 243.0 %copy-start.37 = (pred[32,64]{1,0:T(8,128)(4,1)S(1)}, pred[32,64]{1,0:T(8,128)(4,1)}, u32[]{:S(2)}) copy-start(pred[32,64]{1,0:T(8,128)(4,1)} %copy-done.36) | copy-start | bytes 6148
  6569.3 372.6 %all-to-all-start.2 = ((bf16[4,2,896,16,128]{4,3,2,1,0:T(8,128)(2,1)}), bf16[4,2,896,16,128]{4,3,2,1,0:T(8,128)(2,1)}, u32[]{:S(2)}, u32[]{:S(2)}) async-start(bf16[4,2,896,16,128]{4,3,2,1,0:T(8,128)(2,1)} %get-tuple-element.320), calls=%async_computation.2 | async-start | bytes 58720256 | tf_op jit(solution)/shard_map/all_to_all | solution.py:187
Sparse Core Ops, SparseCore 0:
  9.5 107.0 all-gather.3
  5001.2 385.9 all-gather.5
  5608.2 384.1 all-gather.7
where the time goes:
time: 6990 us; the launch traced here: 6960 us
  local copies, waits for them, and re-layouts  2130 us (30%)
  matrix products  1750 us (25%)
  blocking collectives  1700 us (24%)
  other arithmetic  1270 us (18%)
  waiting for transfers between devices  70.3 us (1%)
    psum x4, blocking collectives, finish_layer(): lax.psum(jnp.dot(context, wo_l, preferred_element_type=jnp.float32), 'tp')  852 us
    psum x4, blocking collectives, finish_layer(): lax.psum(jnp.dot(activated, wd_l, preferred_element_type=jnp.float32), 'tp')  845 us
    scatter x256, other arithmetic  830 us
    slice x2, local copies, waits for them, and re-layouts, layer_weights(): w_gate[layer]  350 us
    unnamed x81, local copies, waits for them, and re-layouts  323 us
    dot_general x4, matrix products, finish_layer(): jnp.dot(activated, wd_l, preferred_element_type=jnp.float32)  281 us
    dot_general x4, matrix products, finish_layer(): jnp.dot(normed, wg_l, preferred_element_type=jnp.float32)  272 us
    slice x4, local copies, waits for them, and re-layouts, layer_weights(): qkv_l[:, :q_cols]  259 us
  transfers between devices with their start and end apart: 6, of which 1 were waited for; matrix products, arithmetic and copies ran while one was open for 35% of the time, Pallas kernels for 0%

commit v1 on v0

v1 whole, which is shorter than its diff:
```python
import jax
import jax.numpy as jnp
from jax import lax
from jax.experimental import pallas as pl
from jax.experimental.pallas import tpu as pltpu
from jax.sharding import PartitionSpec as P

ROPE_BASE = 10000.0
NORM_EPS = 1e-5
NEG = -1e30
BF = jnp.bfloat16
F32 = jnp.float32
ANY = pl.BlockSpec(memory_space=pl.ANY)
SMEM = pl.BlockSpec(memory_space=pltpu.SMEM)
WHOLE = pl.BlockSpec(memory_space=pltpu.VMEM)
VMEM_LIMIT = 61 * 2**20
LOG2E = 1.4426950408889634
LANES = 128
WIDE = 256
CHUNK = 512
HALVES = (0, WIDE)
SUB = 16
PER = 4
EARLY_SENT = 5
dma = pltpu.make_async_copy
sds = jax.ShapeDtypeStruct
sem = pltpu.SemaphoreType.DMA


def at(start, size, multiple=LANES):
    return pl.ds(pl.multiple_of(start, multiple), size)


def cost(flops, size):
    return pl.CostEstimate(flops=flops, bytes_accessed=size, transcendentals=0)


def params(**kw):
    return pltpu.CompilerParams(vmem_limit_bytes=VMEM_LIMIT, **kw)


def remote(src, dst, send, recv, dev):
    return pltpu.make_async_remote_copy(src_ref=src, dst_ref=dst, send_sem=send, recv_sem=recv, device_id=dev, device_id_type=pl.DeviceIdType.MESH)


def meet(devices):
    barrier = pltpu.get_barrier_semaphore()
    for dev in devices:
        pl.semaphore_signal(barrier, device_id=dev, device_id_type=pl.DeviceIdType.MESH)
    pl.semaphore_wait(barrier, len(devices))


def each(count, fn):
    lax.fori_loop(0, count, lambda i, c: (fn(i), c)[1], 0)


def begin(copies):
    for cp in copies:
        cp.start()


def finish_all(copies):
    for cp in copies:
        cp.wait()


def norm_rows(src, dst, base, rows):
    def step(i):
        sl = at(base + i * SUB, SUB, SUB)
        wide = src[sl, :].astype(F32)
        scale = lax.rsqrt(jnp.mean(wide * wide, axis=-1, keepdims=True) + NORM_EPS)
        dst[sl, :] = (wide * scale).astype(BF)
    each(rows // SUB, step)


class Dims:
    def __init__(self, rows, dec, model, heads, head_dim, ff, max_req):
        self.rows, self.half = rows, rows // 2
        self.dec, self.dhalf = dec, dec // 2
        self.blk = self.half + self.dhalf
        self.all = 2 * self.blk
        self.model, self.heads, self.hd, self.ff = model, heads, head_dim, ff
        self.max_req = max_req
        self.loc = heads * head_dim
        self.window = LANES + 2 * rows
        self.lanes = (0, model, LANES)


def front_call(dm, layer, first, ins, w_qkv, tab_c, tab_s, perm, lengths, ends, kc, vc):
    nb = 4
    per_sec = dm.heads // PER
    steps = 3 * per_sec
    kv_steps = 2 * per_sec
    h, d, k = dm.half, dm.dhalf, dm.blk
    m = dm.all if first else k
    npass = dm.all // m
    width = PER * dm.hd
    lead = dm.window - dm.rows
    batch, cache = kc.shape[2], kc.shape[3]
    flat = cache * dm.heads
    ring = 3
    dsteps = batch // PER
    ni = len(ins)

    def kern(*refs):
        rin = refs[:ni]
        (w_ref, c_ref, s_ref, perm_ref, len_ref, end_ref, k_ref, v_ref, kvh, kv3, qh, dec, co, ci, do, di,
         xn, wb, kcat, qv, sd, dv, acc_a, acc_b, bias, sbuf, pbuf, cbuf, cr, dsc, dbuf, dout, o3, stat, raw,
         wsem, isem, csem, tsem, pss, prs, ess, ers, yss, yrs, lss, lrs) = refs[ni:]
        tp = lax.axis_index('tp')
        side = lax.axis_index('side')
        odd = lax.rem(side, 2)
        to_y = {'tp': 1 - tp}

        def wcopies(i):
            slot = lax.rem(i, nb)
            j = lax.rem(i, steps)
            sec = j // per_sec
            base = jnp.where(sec == 2, 0, (sec + 1) * 2 * dm.loc)
            out = []
            for n in range(PER):
                col = base + (2 * (PER * lax.rem(j, per_sec) + n) + tp) * dm.hd
                out.append(dma(w_ref.at[layer, :, at(col, dm.hd)], wb.at[slot, :, pl.ds(n * dm.hd, dm.hd)], wsem.at[slot, n]))
            return out

        def caches(i):
            slot = lax.rem(i, ring)
            b = at(PER * i, PER, PER)
            return [dma(ref.at[0, layer, b], cr.at[slot, n], csem.at[slot, n]) for n, ref in enumerate((k_ref, v_ref))]

        if first:
            parts = [(rin[0], 0, 0, h), (rin[1], 0, h, d), (rin[0], h, k, h), (rin[1], d, k + h, d)]
            loads = [dma(ref.at[pl.ds(src, n)], xn.at[pl.ds(dst, n)], isem.at[i]) for i, (ref, src, dst, n) in enumerate(parts)]
        else:
            own1, own2, peer1, ss_in = rin
            cut = own1.shape[1]
            head_cols, tail_cols = pl.ds(0, cut), pl.ds(cut, dm.model - cut)
            top, low_rows = pl.ds(0, k), pl.ds(k, k)
            loads = [dma(own1, xn.at[top, head_cols], isem.at[0]), dma(own2, xn.at[top, tail_cols], isem.at[1]),
                     dma(ss_in, stat.at[0], isem.at[2]), dma(peer1, xn.at[low_rows, head_cols], isem.at[3]), dma(own2, raw, tsem.at[0])]
        begin(loads)
        for i in range(nb - 1):
            begin(wcopies(jnp.int32(i)))
        begin(caches(jnp.int32(0)))

        def zero(i):
            kcat[:, i, pl.ds(0, lead), :] = jnp.zeros((2, lead, dm.hd), BF)
        each(dm.heads, zero)
        meet([{'side': lax.rem(side + i, 4)} for i in range(1, 4)] + [to_y])
        late = []
        if not first:
            loads[4].wait()
            late = [remote(raw, xn.at[low_rows, tail_cols], lss.at[0], lrs.at[0], to_y),
                    remote(ss_in, stat.at[1], lss.at[1], lrs.at[1], to_y)]
            begin(late[::-1])

        def own_part(j):
            return kcat.at[j // per_sec, at(PER * lax.rem(j, per_sec), PER, PER), pl.ds(lead, dm.rows)]

        def edge_part(j, row):
            return kcat.at[j // per_sec, at(PER * lax.rem(j, per_sec), PER, PER), pl.ds(row, LANES)]

        def peer_copy(j):
            dst = kcat.at[j // per_sec, at(PER * lax.rem(j, per_sec), PER, PER), pl.ds(LANES, dm.rows)]
            return remote(own_part(j), dst, pss.at[j], prs.at[j], {'side': side + 1})

        def edge_copy(j, to):
            row = dm.window - LANES if to == 2 else dm.rows
            return remote(edge_part(j, row), edge_part(j, (3 - to) * dm.rows), ess.at[j], ers.at[j], {'side': to})

        def send(j):
            pl.when(odd == 0)(lambda: peer_copy(j).start())
            pl.when(side == 1)(lambda: edge_copy(j, 2).start())

        def arrived(j):
            pl.when(odd == 1)(lambda: peer_copy(j).wait_recv())

            @pl.when(side == 2)
            def _():
                edge_copy(j, 2).wait_recv()
                edge_copy(j, 3).start()
            pl.when(side == 3)(lambda: edge_copy(j, 3).wait_recv())

        def sent(j):
            pl.when(odd == 0)(lambda: peer_copy(j).wait_send())
            pl.when(side == 1)(lambda: edge_copy(j, 2).wait_send())
            pl.when(side == 2)(lambda: edge_copy(j, 3).wait_send())

        def dots(i, rows, acc):
            @pl.when(i + nb - 1 < npass * steps)
            def _():
                begin(wcopies(i + nb - 1))
            finish_all(wcopies(i))
            acc[...] = jnp.dot(xn[rows, :], wb[lax.rem(i, nb)], preferred_element_type=F32)

        def epilogue(j, acc, blocks, is_q):
            sec, jj = j // per_sec, lax.rem(j, per_sec)
            for r0, b in blocks:
                rows = slice(r0, r0 + k)
                cv, sv = c_ref[at(b * k, k, SUB), :], s_ref[at(b * k, k, SUB), :]
                for n in range(PER):
                    head = PER * jj + n
                    val = acc[rows, n * dm.hd:(n + 1) * dm.hd].astype(BF).astype(F32)
                    rot = val * cv + pltpu.roll(val, dm.hd // 2, 1) * sv
                    low = (rot if is_q else jnp.where(sec == 1, val, rot)).astype(BF)
                    if is_q:
                        qv[head, at(b * h, h, SUB), :] = low[:h]
                    else:
                        kcat[sec, head, at(lead + b * h, h, SUB), :] = low[:h]
                    sd[sec, head, at(b * d, d, d), :] = low[h:]

        def run(p, blocks):
            rows = pl.ds(p * m, m)
            base = p * steps
            final = p == npass - 1
            last = kv_steps

            def done(j):
                if final:
                    pl.when(j > 0)(lambda: send(j - 1))

            dots(jnp.int32(base), rows, acc_a)

            def pair(q):
                dots(base + 2 * q + 1, rows, acc_b)
                epilogue(2 * q, acc_a, blocks, False)
                done(2 * q)
                dots(base + 2 * q + 2, rows, acc_a)
                epilogue(2 * q + 1, acc_b, blocks, False)
                done(2 * q + 1)
            each(last // 2 - 1, pair)
            dots(jnp.int32(base + last - 1), rows, acc_b)
            epilogue(jnp.int32(last - 2), acc_a, blocks, False)
            done(jnp.int32(last - 2))
            if final:
                epilogue(jnp.int32(last - 1), acc_b, blocks, False)
                done(jnp.int32(last - 1))
                return
            dots(jnp.int32(base + last), rows, acc_a)
            epilogue(jnp.int32(last - 1), acc_b, blocks, False)
            for n in range(1, per_sec):
                prev, acc = (acc_a, acc_b) if n % 2 else (acc_b, acc_a)
                dots(jnp.int32(base + last + n), rows, acc)
                epilogue(jnp.int32(last + n - 1), prev, blocks, True)
            epilogue(jnp.int32(steps - 1), acc, blocks, True)

        def apply_norm(n, base):
            total_sq = jnp.sum(stat[n], axis=1, keepdims=True)
            stat[n] = jnp.broadcast_to(lax.rsqrt(total_sq / dm.model + NORM_EPS), (k, LANES))

            def step(i):
                sl = at(base + i * SUB, SUB, SUB)
                for c in range(*dm.lanes):
                    xn[sl, c:c + LANES] = (xn[sl, c:c + LANES].astype(F32) * stat[n, at(i * SUB, SUB, SUB), :]).astype(BF)
            each(k // SUB, step)

        if first:
            finish_all(loads)
            norm_rows(xn, xn, 0, m)
            blocks = [(0, 0), (k, 1)]
        else:
            finish_all(loads[:3])
            apply_norm(0, 0)
            run(0, [(0, tp)])
            loads[3].wait()
            finish_all(late)
            apply_norm(1, k)
            blocks = [(0, 1 - tp)]
        run(npass - 1, blocks)

        def cols(g):
            return at(width * g, width)

        def ctx_send(g):
            return remote(cbuf.at[0, :, cols(g)], ci.at[:, cols(g)], yss.at[g], yrs.at[g], to_y)

        dec_send = remote(dout.at[at((1 - tp) * d, d, SUB)], di, yss.at[per_sec], yrs.at[per_sec], to_y)
        dec_keep = dma(dout.at[at(tp * d, d, SUB)], do, isem.at[0])

        def score(b, w, head, n):
            sbuf[n % 2, :, :w] = lax.dot_general(qv[head, b * h:(b + 1) * h, :], kcat[0, head, :w, :], (((1,), (1,)), ((), ())), preferred_element_type=F32)

        def value(ph, w, head, n):
            s = sbuf[n % 2, :, :w] * (dm.hd ** -0.5 * LOG2E) + bias[:, :w]
            p = jnp.exp2(s - jnp.max(s, axis=1, keepdims=True))
            pbuf[n % 2, :, :w] = p.astype(BF)
            tot = jnp.sum(p, axis=1, keepdims=True)
            o = jnp.dot(pbuf[n % 2, :, :w], kcat[1, head, :w, :], preferred_element_type=F32)
            cbuf[ph, :, at(head * dm.hd, dm.hd)] = (o / tot).astype(BF)

        def turn_rows(rows, out):
            x = jnp.concatenate([r.reshape(SUB * dm.heads, dm.hd) for r in rows], axis=1)
            y = jnp.dot(perm_ref[...], x, preferred_element_type=F32).astype(BF)
            for n, dst in enumerate(out):
                dst(y[:, n * dm.hd:(n + 1) * dm.hd].reshape(SUB, dm.heads, dm.hd))

        def decode():
            col = lax.broadcasted_iota(jnp.int32, (dm.heads, flat), 1)
            row = lax.broadcasted_iota(jnp.int32, (dm.heads, flat), 0)
            pos = jnp.where(lax.rem(col, dm.heads) == row, col // dm.heads, flat)
            scale = dm.hd ** -0.5

            def look(i, par):
                @pl.when(i + 1 < dsteps)
                def _():
                    begin(caches(i + 1))
                finish_all(caches(i))
                for n in range(PER):
                    keys = cr[lax.rem(i, ring), 0, n].reshape(flat, dm.hd)
                    dsc[par, n] = lax.dot_general(dv[2, PER * i + n], keys, (((1,), (1,)), ((), ())), preferred_element_type=F32)

            def gather(i, par):
                for n in range(PER):
                    bi = PER * i + n
                    q, kn, vn = dv[2, bi].astype(F32), dv[0, bi].astype(F32), dv[1, bi].astype(F32)
                    s = jnp.where(pos < len_ref[bi], dsc[par, n] * scale, NEG)
                    fresh = jnp.sum(q * kn, axis=1, keepdims=True) * scale
                    top = jnp.maximum(jnp.max(s, axis=1, keepdims=True), fresh)
                    p = jnp.exp(s - top)
                    pf = jnp.exp(fresh - top)
                    inv = 1.0 / (jnp.sum(p, axis=1, keepdims=True) + pf)
                    vals = cr[lax.rem(i, ring), 1, n].reshape(flat, dm.hd)
                    o = jnp.dot((p * inv).astype(BF), vals, preferred_element_type=F32)
                    dbuf[bi] = o + (pf * inv).astype(BF).astype(F32) * vn

            look(jnp.int32(0), 0)

            def two(t):
                look(2 * t + 1, 1)
                gather(2 * t, 0)
                look(2 * t + 2, 0)
                gather(2 * t + 1, 1)
            each(dsteps // 2 - 1, two)
            look(jnp.int32(dsteps - 1), 1)
            gather(jnp.int32(dsteps - 2), 0)
            gather(jnp.int32(dsteps - 1), 1)
            for n in range(dm.heads):
                dout[:, n * dm.hd:(n + 1) * dm.hd] = dbuf[:, n, :].astype(BF)

        def put(ref, *idx):
            def store(val):
                ref[idx] = val
            return store

        def turn_all():
            def block(i):
                for n in range(PER):
                    row = (PER * i + n) * SUB
                    sl, own = at(row, SUB, SUB), at(lead + row, SUB, SUB)
                    turn_rows([kcat[0, :, own, :], kcat[1, :, own, :]], [put(o3, 0, sl), put(o3, 1, sl)])
            each(dm.rows // SUB // PER, block)

        kv3_copy = dma(o3, kv3, tsem.at[0])
        kvh_copy = dma(kcat.at[:, :, pl.ds(lead, dm.rows)], kvh, tsem.at[1])
        q_copy = dma(qv, qh, tsem.at[2])
        dec_copy = dma(dv, dec, tsem.at[3])

        def stage(t):
            ph, g = t // per_sec, lax.rem(t, per_sec)
            b = lax.rem(1 + tp + ph, 2)

            @pl.when(ph == 0)
            def _():
                dots(npass * steps - per_sec + g, pl.ds((npass - 1) * m, m), acc_a)
                epilogue(kv_steps + g, acc_a, blocks, True)
                pl.when(g == 0)(lambda: send(kv_steps - 1))
                arrived(g)
                arrived(per_sec + g)

            @pl.when(t == per_sec)
            def _():
                for i in range(dm.dec // SUB):
                    sl = pl.ds(i * SUB, SUB)
                    turn_rows([sd[n, :, sl, :] for n in range(3)], [put(dv, n, sl) for n in range(3)])
                turn_all()
                begin([kv3_copy, kvh_copy, q_copy, dec_copy])
                ctx_send(per_sec - 1).start()
                decode()

            @pl.when(g == 0)
            def _():
                row0 = dm.rows * side + h * b
                for c in range(dm.window // LANES):
                    rows = row0 + lax.broadcasted_iota(jnp.int32, (h, LANES), 0)
                    col = dm.rows * side - lead + c * LANES + lax.broadcasted_iota(jnp.int32, (h, LANES), 1)
                    start = jnp.zeros_like(rows)
                    for r in range(4):
                        start = jnp.where(rows >= end_ref[r], end_ref[r], start)
                    bias[:, c * LANES:(c + 1) * LANES] = jnp.where((col >= start) & (col <= rows), 0.0, NEG)
            pl.when(t == per_sec)(lambda: begin([dec_send, dec_keep]))

            for bb, w in enumerate((dm.window - h, dm.window)):
                @pl.when(b == bb)
                def _(bb=bb, w=w):
                    score(bb, w, PER * g, 0)
                    for n in range(PER):
                        if n + 1 < PER:
                            score(bb, w, PER * g + n + 1, n + 1)
                        value(ph, w, PER * g + n, n)
            pl.when((ph == 0) & (g > 0))(lambda: ctx_send(g - 1).start())
        each(2 * per_sec, stage)

        keep = dma(cbuf.at[1], co, isem.at[1])
        keep.start()
        each(kv_steps, sent)
        finish_all([kv3_copy, kvh_copy, q_copy, dec_copy, dec_keep, dec_send])
        each(per_sec, lambda g: ctx_send(g).wait())
        keep.wait()

    heads = (dm.heads, dm.rows, dm.hd)
    three = (dm.heads, dm.hd)
    flops = 2 * dm.all * dm.model * width * steps
    outs = [(2,) + heads, (2, dm.rows) + three, heads, (3, dm.dec) + three, (h, dm.loc), (h, dm.loc), (d, dm.loc), (d, dm.loc)]
    acc = pltpu.VMEM((m, width), F32)
    vec = sem((kv_steps,))
    return pl.pallas_call(
        kern, out_shape=tuple(sds(s, BF) for s in outs),
        in_specs=[ANY] * (ni + 1) + [WHOLE] * 3 + [SMEM] * 2 + [ANY] * 2, out_specs=(ANY,) * len(outs),
        scratch_shapes=[
            pltpu.VMEM((dm.all, dm.model), BF), pltpu.VMEM((nb, dm.model, width), BF), pltpu.VMEM((2, dm.heads, dm.window, dm.hd), BF),
            pltpu.VMEM(heads, BF), pltpu.VMEM((3, dm.heads, dm.dec, dm.hd), BF), pltpu.VMEM((3, dm.dec) + three, BF), acc, acc,
            pltpu.VMEM((h, dm.window), F32), pltpu.VMEM((2, h, dm.window), F32), pltpu.VMEM((2, h, dm.window), BF), pltpu.VMEM((2, h, dm.loc), BF),
            pltpu.VMEM((ring, 2, PER, cache) + three, BF), pltpu.VMEM((2, PER, dm.heads, flat), F32), pltpu.VMEM((batch,) + three, F32),
            pltpu.VMEM((batch, dm.loc), BF), pltpu.VMEM((2, dm.rows) + three, BF), pltpu.VMEM((2, k, LANES), F32), pltpu.VMEM((k, dm.model - EARLY_SENT * CHUNK), BF),
            sem((nb, PER)), sem((4,)), sem((ring, 2)), sem((4,)), vec, vec, vec, vec,
            sem((per_sec + 1,)), sem((per_sec + 1,)), sem((2,)), sem((2,))],
        compiler_params=params(collective_id=layer, has_side_effects=True),
        cost_estimate=cost(flops, dm.model * width * steps * 2),
        name="front")(*ins, w_qkv, tab_c, tab_s, perm, lengths, ends, kc, vc)


def general_attention(dm, meta, qh, kvs):
    nk = LANES + 4 * dm.rows
    groups = dm.heads // PER
    hb = dm.half
    wmax = dm.max_req + hb + WIDE

    def kern(meta_ref, q_ref, *refs):
        srcs = refs[:4]
        o_ref, kcat, sc, bias, mx, ls, pv, lsem = refs[4:]
        g = pl.program_id(0)
        side = lax.axis_index('side')
        row0 = dm.rows * side + hb * meta_ref[0]
        copies = [dma(ref.at[:, at(PER * g, PER, PER)], kcat.at[:, :, at(LANES + dm.rows * (side ^ n), dm.rows)], lsem.at[n]) for n, ref in enumerate(srcs)]
        kcat[:, :, :LANES, :] = jnp.zeros((2, PER, LANES, dm.hd), BF)
        begin(copies)

        def seg_start(row):
            st = jnp.zeros_like(row)
            for r in range(4):
                st = jnp.where(row >= meta_ref[1 + r], meta_ref[1 + r], st)
            return st

        n = (row0 + hb - seg_start(row0) // LANES * LANES + WIDE - 1) // WIDE
        begin_col = row0 + hb - WIDE * n
        rows = row0 + lax.broadcasted_iota(jnp.int32, (hb, WIDE), 0)
        st_rows = seg_start(rows)
        lanes = lax.broadcasted_iota(jnp.int32, (hb, WIDE), 1)
        mx[...] = jnp.full_like(mx, NEG)
        ls[...] = jnp.zeros_like(ls)
        pv[...] = jnp.zeros_like(pv)
        finish_all(copies)

        def scores(c):
            first = begin_col + WIDE * c
            col = first + lanes
            bias[...] = jnp.where((col >= st_rows) & (col <= rows), 0.0, NEG)
            for i in range(PER):
                keys = kcat[0, i, at(LANES + first, WIDE), :]
                s = lax.dot_general(q_ref[i], keys, (((1,), (1,)), ((), ())), preferred_element_type=F32)
                s = s * (dm.hd ** -0.5 * LOG2E) + bias[...]
                sc[i, :, at(c * WIDE, WIDE)] = s
                mx[i] = jnp.maximum(mx[i], jnp.max(s, axis=1, keepdims=True))
        each(n, scores)

        def values(c):
            for i in range(PER):
                p = jnp.exp2(sc[i, :, at(c * WIDE, WIDE)] - mx[i][:, :1])
                ls[i] += jnp.sum(p, axis=1, keepdims=True)
                vals = kcat[1, i, at(LANES + begin_col + WIDE * c, WIDE), :]
                pv[i] += jnp.dot(p.astype(BF), vals, preferred_element_type=F32)
        each(n, values)
        for i in range(PER):
            o_ref[:, i * dm.hd:(i + 1) * dm.hd] = (pv[i] / ls[i]).astype(BF)

    stat = pltpu.VMEM((PER, hb, LANES), F32)
    grid_spec = pltpu.PrefetchScalarGridSpec(
        num_scalar_prefetch=1, grid=(groups,),
        in_specs=[pl.BlockSpec((PER, hb, dm.hd), lambda g, mt: (g, mt[0], 0))] + [ANY] * 4,
        out_specs=pl.BlockSpec((hb, PER * dm.hd), lambda g, mt: (0, g)),
        scratch_shapes=[pltpu.VMEM((2, PER, nk, dm.hd), BF), pltpu.VMEM((PER, hb, wmax), F32), pltpu.VMEM((hb, WIDE), F32), stat, stat, stat, sem((4,))])
    return pl.pallas_call(
        kern, out_shape=sds((hb, dm.loc), BF), grid_spec=grid_spec,
        compiler_params=params(dimension_semantics=("arbitrary",)), name="general_attn")(meta, qh, *kvs)


def post_call(dm, layer, first, resid, co, do, ci, di, kv3, w_out, w_gate, w_up, w_down):
    nb = 6
    kc = dm.model
    ffh = dm.ff // 2
    n_out = dm.model // CHUNK
    n_full = ffh // WIDE
    rem = ffh - n_full * WIDE
    n_gu = n_full + 1
    n_dn = n_out
    ksz = [kc, ffh - kc]
    nk = len(ksz)
    gu0, dn0 = n_out, n_out + n_gu
    total = dn0 + n_dn * nk
    assert rem and n_full % 2
    m = dm.blk
    h, d = dm.half, dm.dhalf
    crow = dm.rows // n_dn
    nr = len(resid)
    cut = EARLY_SENT * CHUNK

    def kern(*refs):
        rin = refs[:nr]
        (co_r, do_r, ci_r, di_r, kv, wo, wg, wu, wd, oa, ot, ob, os, kvx, kvp, kvq,
         h1, h1p, xn, act, tmp, wb, acc_a, acc_b, psend, precv, pown, ss, ssp,
         wsem, isem, osem, hss, hrs, pss, prs, yss, yrs, xss, xrs, fss, frs, dss, drs) = refs[nr:]
        tp = lax.axis_index('tp')
        side = lax.axis_index('side')
        core = lax.rem(side, 2)
        to_core = {'side': side + 1 - 2 * core}
        to_x = {'side': lax.rem(side + 2, 4)}
        to_y = {'tp': 1 - tp}

        def cols(j):
            return at(j * CHUNK, CHUNK)

        def block(i, fn):
            slot = lax.rem(i, nb)

            @pl.when(i < gu0)
            def _():
                fn(dma(wo.at[layer, :, cols(i)], wb.at[slot], wsem.at[slot, 0]))

            for on, w in (((i >= gu0) & (i < dn0 - 1), WIDE), (i == dn0 - 1, rem)):
                @pl.when(on)
                def _(w=w):
                    c = at(core * ffh + (i - gu0) * WIDE, w)
                    for n, ref in enumerate((wg, wu)):
                        fn(dma(ref.at[layer, :, c], wb.at[slot, :, pl.ds(n * w, w)], wsem.at[slot, n]))

            j = i - dn0
            for n in range(nk):
                @pl.when((j >= 0) & (i < total) & (lax.rem(j, nk) == n))
                def _(n=n):
                    r = at(core * ffh + n * kc, ksz[n])
                    fn(dma(wd.at[layer, r, cols(j // nk)], wb.at[slot, pl.ds(0, ksz[n])], wsem.at[slot, 0]))

        def start(i):
            block(i, lambda c: c.start())

        def wait(i):
            block(i, lambda c: c.wait())

        mine, theirs = at(tp * h, h, SUB), at(tp * d, d, SUB)
        head_rows, tail_rows = pl.ds(0, h), pl.ds(h, d)
        pairs = [(co_r, tmp.at[0, head_rows]), (do_r, tmp.at[0, tail_rows]), (ci_r, tmp.at[1, head_rows]), (di_r, tmp.at[1, tail_rows])]
        if first:
            pairs += [(rin[0].at[mine], h1.at[head_rows]), (rin[1].at[theirs], h1.at[tail_rows])]
        else:
            pairs += [(rin[0], h1.at[:, pl.ds(0, cut)]), (rin[1], h1.at[:, pl.ds(cut, dm.model - cut)])]
        loads = [dma(a, b, isem.at[n]) for n, (a, b) in enumerate(pairs)]
        begin(loads)
        for i in range(nb - 1):
            start(jnp.int32(i))
        meet([to_core, to_x, to_y])

        def bulk(i):
            r = at(i * crow, crow, SUB)
            return remote(kv.at[:, r], kvx.at[:, r], xss.at[i], xrs.at[i], to_x)

        def forward(i):
            r = at(i * crow, crow, SUB)
            return remote(kvx.at[:, r], kvq.at[:, r], fss.at[i], frs.at[i], to_core)

        near = remote(kv, kvp, dss.at[0], drs.at[0], to_core)
        each(n_dn, lambda i: bulk(i).start())
        finish_all(loads)
        for i in range(dm.heads):
            for n, t in enumerate((tp, 1 - tp)):
                xn[:m, at((2 * i + t) * dm.hd, dm.hd)] = tmp[n, :, i * dm.hd:(i + 1) * dm.hd]
        ss[...] = jnp.zeros_like(ss)

        def hsend(j):
            return remote(h1.at[:, cols(j)], h1p.at[:, cols(j)], hss.at[j], hrs.at[j], to_core)

        ss_send = remote(ss, ssp, dss.at[1], drs.at[1], to_core)

        def add_to_hidden(cs, acc):
            out = (h1[:, cs].astype(F32) + acc.astype(BF).astype(F32)).astype(BF)
            h1[:, cs] = out
            return out.astype(F32)

        def out_step(i):
            pl.when(i > 0)(lambda: hsend(i - 1).start())
            start(i + nb - 1)
            wait(i)
            slot = lax.rem(i, nb)
            for n in HALVES:
                acc = jnp.dot(xn[:m, :], wb[slot, :, n:n + WIDE], preferred_element_type=F32)
                out = add_to_hidden(at(i * CHUNK + n, WIDE), acc)
                ss[...] += out[:, :LANES] * out[:, :LANES] + out[:, LANES:] * out[:, LANES:]
        each(n_out, out_step)

        def apply_norm(src, stat, base):
            total_sq = jnp.sum(stat[...], axis=1, keepdims=True)
            stat[...] = jnp.broadcast_to(lax.rsqrt(total_sq / dm.model + NORM_EPS), stat.shape)

            def step(i):
                sl = at(i * SUB, SUB, SUB)
                for c in range(*dm.lanes):
                    xn[at(base + i * SUB, SUB, SUB), c:c + LANES] = (src[sl, c:c + LANES].astype(F32) * stat[sl, :]).astype(BF)
            each(m // SUB, step)

        ss_send.start()
        hsend(n_out - 1).start()
        ss_send.wait_send()
        apply_norm(h1, ss, 0)
        ss_send.wait_recv()
        each(n_out, lambda j: hsend(j).wait_recv())
        near.start()
        apply_norm(h1p, ssp, m)

        def dots(i, acc):
            start(i + nb - 1)
            wait(i)
            acc[...] = jnp.dot(xn[...], wb[lax.rem(i, nb)], preferred_element_type=F32)

        def glu(acc, j, w):
            gate = acc[:, :w].astype(BF).astype(F32)
            upper = acc[:, w:2 * w].astype(BF).astype(F32)
            act[:, at(j * WIDE, w)] = (jax.nn.silu(gate) * upper).astype(BF)

        dots(jnp.int32(gu0), acc_a)

        def gu_pair(q):
            dots(gu0 + 2 * q + 1, acc_b)
            glu(acc_a, 2 * q, WIDE)
            dots(gu0 + 2 * q + 2, acc_a)
            glu(acc_b, 2 * q + 1, WIDE)
        each(n_full // 2, gu_pair)
        start(jnp.int32(dn0 - 1 + nb - 1))
        wait(jnp.int32(dn0 - 1))
        acc_b[:, :2 * rem] = jnp.dot(xn[...], wb[(dn0 - 1) % nb, :, :2 * rem], preferred_element_type=F32)
        glu(acc_a, n_full - 1, WIDE)
        glu(acc_b, n_full, rem)

        def share(j):
            return remote(h1.at[:, cols(j)], ob.at[:, cols(j)], yss.at[j], yrs.at[j], to_y)

        def keeps(j, fn):
            @pl.when(j < EARLY_SENT)
            def _():
                fn(dma(h1.at[:, cols(j)], oa.at[:, cols(j)], osem.at[j]))

            @pl.when(j >= EARLY_SENT)
            def _():
                fn(dma(h1.at[:, cols(j)], ot.at[:, cols(j - EARLY_SENT)], osem.at[j]))

        def deliver(j):
            keeps(j, lambda c: c.start())
            pl.when(j < EARLY_SENT)(lambda: share(j).start())

        def psend_copy(j):
            return remote(psend.at[lax.rem(j, 2)], precv.at[j], pss.at[j], prs.at[j], to_core)

        def finish(j):
            for n in HALVES:
                out = add_to_hidden(at(j * CHUNK + n, WIDE), pown[lax.rem(j, 2), :, n:n + WIDE] + precv[j, :, n:n + WIDE])
                ss[...] += out[:, :LANES] * out[:, :LANES] + out[:, LANES:] * out[:, LANES:]

        def part(rows, slots, n):
            return sum(jnp.dot(act[rows, i * kc:i * kc + ksz[i]], wb[slots[i], :ksz[i], n:n + WIDE], preferred_element_type=F32) for i in range(nk))

        def down(j, first):
            i0 = dn0 + j * nk
            if not first:
                start(i0 + nb - 2)
            start(i0 + nb - 1)
            slots = []
            for n in range(nk):
                wait(i0 + n)
                slots.append(lax.rem(i0 + n, nb))
            half = lax.rem(j, 2)
            pl.when(j > 1)(lambda: psend_copy(j - 2).wait_send())
            for n in HALVES:
                psend[half, :, n:n + WIDE] = part(slice(m, 2 * m), slots, n)
            if not first:
                psend_copy(j - 1).wait_recv()
            psend_copy(j).start()
            if not first:
                finish(j - 1)
            for n in HALVES:
                pown[half, :, n:n + WIDE] = part(slice(0, m), slots, n)
            if not first:
                deliver(j - 1)
            bulk(j).wait_recv()
            forward(j).start()

        each(n_out, lambda j: hsend(j).wait_send())
        ss[...] = jnp.zeros_like(ss)
        down(jnp.int32(0), True)
        each(n_dn - 1, lambda j: down(j + 1, False))
        psend_copy(n_dn - 1).wait_recv()
        finish(n_dn - 1)
        for j in (n_dn - 2, n_dn - 1):
            psend_copy(j).wait_send()
        near.wait()
        deliver(n_dn - 1)
        ss_keep = dma(ss, os, isem.at[0])
        ss_keep.start()
        ss_keep.wait()

        def last(j):
            bulk(j).wait_send()
            forward(j).wait()
            keeps(j, lambda c: c.wait())
            pl.when(j < EARLY_SENT)(lambda: share(j).wait())
        each(n_dn, last)

    part1, part2 = sds((m, cut), BF), sds((m, dm.model - cut), BF)
    two = sds(kv3.shape, BF)
    acc = pltpu.VMEM((2 * m, CHUNK), F32)
    pair = pltpu.VMEM((2, m, CHUNK), F32)
    vec = sem((n_dn,))
    stat = pltpu.VMEM((m, LANES), F32)
    return pl.pallas_call(
        kern, out_shape=(part1, part2, part1, sds((m, LANES), F32), two, two, two),
        in_specs=[ANY] * (nr + 9), out_specs=(ANY,) * 7,
        scratch_shapes=[
            pltpu.VMEM((m, dm.model), BF), pltpu.VMEM((m, dm.model), BF), pltpu.VMEM((2 * m, dm.model), BF),
            pltpu.VMEM((2 * m, ffh), BF), pltpu.VMEM((2, m, dm.loc), BF), pltpu.VMEM((nb, kc, CHUNK), BF),
            acc, acc, pair, pltpu.VMEM((n_dn, m, CHUNK), F32), pair, stat, stat,
            sem((nb, 2)), sem((6,)), vec, vec, vec, vec, vec, vec, vec, vec, vec, vec, vec, sem((2,)), sem((2,))],
        compiler_params=params(collective_id=2 + layer, has_side_effects=True),
        cost_estimate=cost(2 * m * dm.model * (dm.model + 3 * dm.ff), dm.model * (2 * dm.model + 3 * dm.ff)),
        name="post")(*resid, co, do, ci, di, kv3, w_out, w_gate, w_up, w_down)


def tail_call(dm, meta, lengths, kv3, news, kc, vc):
    layers, batch, cache = kc.shape[1:4]
    bits = [1 << b for b in reversed(range(dm.rows.bit_length()))]
    nsrc = len(kv3[0])
    per_layer = batch // PER
    steps = layers * per_layer
    ring = 6
    lag = 2

    def kern(meta_ref, len_ref, *refs):
        srcs, refs = refs[:layers * nsrc], refs[layers * nsrc:]
        dec, refs = refs[:layers], refs[layers:]
        kc_ref, vc_ref, ko, vo, kn, vn, buf, slots, dv, lsem, osem, dsem, isem, wsem = refs
        side = lax.axis_index('side')
        start, length = meta_ref[0], meta_ref[1]

        def pieces(fn):
            for k in range(nsrc):
                first = dm.rows * (side ^ k)
                lo = jnp.maximum(start, first)
                cnt = jnp.maximum(jnp.minimum(start + length, first + dm.rows) - lo, 0)
                for n, bit in enumerate(bits):
                    @pl.when((cnt & bit) != 0)
                    def _(k=k, n=n, bit=bit, first=first, lo=lo, cnt=cnt):
                        off = cnt // (2 * bit) * (2 * bit)
                        for l in range(layers):
                            fn(dma(srcs[l * nsrc + k].at[:, pl.ds(lo - first + off, bit)], buf.at[l, :, pl.ds(lo - start + off, bit)], lsem.at[l, k, n]))

        def spot(i):
            return i // per_layer, at(PER * lax.rem(i, per_layer), PER, PER), lax.rem(i, ring)

        def read(i):
            lay, b, slot = spot(i)
            return [dma(ref.at[0, lay, b], slots.at[slot, n], isem.at[slot, n]) for n, ref in enumerate((kc_ref, vc_ref))]

        def write(i):
            lay, b, slot = spot(i)
            return [dma(slots.at[slot, n], ref.at[0, lay, b], wsem.at[slot, n]) for n, ref in enumerate((kn, vn))]

        dloads = [dma(ref, dv.at[n], dsem.at[n]) for n, ref in enumerate(dec)]
        begin(dloads)
        pieces(lambda c: c.start())
        for i in range(ring - lag):
            begin(read(jnp.int32(i)))

        def zero(r, c):
            buf[:, :, r] = jnp.zeros((layers, 2, dm.heads, dm.hd), BF)
            return c
        lax.fori_loop(length, dm.max_req, zero, 0)
        finish_all(dloads)
        pieces(lambda c: c.wait())
        outs = [dma(buf.at[l, n], ref.at[0, l], osem.at[l, n]) for l in range(layers) for n, ref in enumerate((ko, vo))]
        begin(outs)

        def step(i):
            lay, _, slot = spot(i)
            finish_all(read(i))
            for n in range(PER):
                b = PER * lax.rem(i, per_layer) + n
                for kind in range(2):
                    slots[slot, kind, n, len_ref[b]] = dv[lay, kind, b]
            pl.when(i > 0)(lambda: begin(write(i - 1)))

            @pl.when(i + ring - lag < steps)
            def _():
                pl.when(i >= lag)(lambda: finish_all(write(i - lag)))
                begin(read(i + ring - lag))
        each(steps, step)
        begin(write(jnp.int32(steps - 1)))
        each(ring, lambda i: finish_all(write(steps - ring + i)))
        finish_all(outs)

    shape = sds((1, layers, dm.max_req, dm.heads, dm.hd), BF)
    three = (dm.heads, dm.hd)
    flat = [ref for group in kv3 for ref in group]
    pair = sem((layers, 2))
    return pl.pallas_call(
        kern, out_shape=(shape, shape, sds(kc.shape, BF), sds(vc.shape, BF)),
        in_specs=[SMEM, SMEM] + [ANY] * (len(flat) + layers + 2), out_specs=(ANY,) * 4,
        scratch_shapes=[pltpu.VMEM((layers, 2, dm.max_req) + three, BF), pltpu.VMEM((ring, 2, PER, cache) + three, BF), pltpu.VMEM((layers,) + news[0].shape, BF),
                        sem((layers, nsrc, len(bits))), pair, sem((layers,)), sem((ring, 2)), sem((ring, 2))],
        compiler_params=params(),
        cost_estimate=cost(10**11, kc.size),
        name="tail")(meta, lengths, *flat, *news, kc, vc)


def close_call(dm, mine, theirs):
    cut = mine[0].shape[1]
    h, d, k = dm.half, dm.dhalf, dm.blk

    def kern(a1, a2, b1, b2, hid, dec, buf, lsem, osem):
        tp = lax.axis_index('tp')
        loads = []
        for n, (ref, blk, col) in enumerate(((a1, tp, 0), (a2, tp, cut), (b1, 1 - tp, 0), (b2, 1 - tp, cut))):
            loads.append(dma(ref, buf.at[at(blk * k, k, SUB), pl.ds(col, ref.shape[1])], lsem.at[n]))
        begin(loads)
        finish_all(loads)
        outs = []
        for n in range(2):
            outs.append(dma(buf.at[pl.ds(n * k, h)], hid.at[pl.ds(n * h, h)], osem.at[2 * n]))
            outs.append(dma(buf.at[pl.ds(n * k + h, d)], dec.at[pl.ds(n * d, d)], osem.at[2 * n + 1]))
        begin(outs)
        finish_all(outs)

    return pl.pallas_call(
        kern, out_shape=(sds((dm.rows, dm.model), BF), sds((dm.dec, dm.model), BF)),
        in_specs=[ANY] * 4, out_specs=(ANY, ANY),
        scratch_shapes=[pltpu.VMEM((dm.all, dm.model), BF), sem((4,)), sem((4,))],
        compiler_params=params(), name="close")(*mine, *theirs)


def solution(mesh):
    tp_size = mesh.shape['tp']
    side_size = mesh.shape['side']
    rows_spec = P(('pair', 'side'), None)
    batch_spec = P(('pair', 'side'), None, None)
    cache_spec = P(('pair', 'side'), None, None, None, 'tp', None)
    prompt_spec = P(('pair', 'side'), None, None, 'tp', None)

    def swap(val, axis, bit):
        size = tp_size if axis == 'tp' else side_size
        return lax.ppermute(val, axis, [(i, i ^ bit) for i in range(size)])

    def local_step(x_loc, req_len, dest, w_qkv, w_out, w_gate, w_up, w_down, y_loc, kc, vc, clen_loc):
        side = lax.axis_index('side')
        tp = lax.axis_index('tp')
        layers = w_qkv.shape[0]
        rows = x_loc.shape[0]
        y = y_loc[0]
        lengths = clen_loc[0]
        dm = Dims(rows, y.shape[0], x_loc.shape[1], kc.shape[-2], kc.shape[-1], w_gate.shape[2], 2 * rows - rows // 4)
        h, d = dm.half, dm.dhalf

        ends = jnp.sum(jnp.where(jnp.arange(side_size)[:, None] >= jnp.arange(side_size)[None, :], req_len[None, :], 0), axis=1)
        row_ids = rows * side + jnp.arange(rows)
        seg_start = jnp.max(jnp.where(row_ids[:, None] >= ends[None, :], ends[None, :], 0), axis=1)
        pos = row_ids - seg_start
        positions = jnp.concatenate([pos[:h], lengths[:d], pos[h:], lengths[d:]]).astype(F32)
        half_dim = dm.hd // 2
        inv_freq = ROPE_BASE ** (-jnp.arange(half_dim, dtype=F32) / half_dim)
        angles = positions[:, None] * inv_freq[None, :]
        cos_val, sin_val = jnp.cos(angles), jnp.sin(angles)
        tab_c = jnp.concatenate([cos_val, cos_val], axis=1)
        tab_s = jnp.concatenate([-sin_val, sin_val], axis=1)

        mine = dest == side
        inst_meta = jnp.stack([jnp.sum(jnp.where(mine, ends - req_len, 0)), jnp.sum(jnp.where(mine, req_len, 0))])
        mid = rows * side_size // 2
        fast = mid - jnp.max(jnp.where(ends <= mid, ends, 0)) <= LANES

        span = SUB * dm.heads
        src = jnp.arange(span)
        perm = ((src % dm.heads * SUB + src // dm.heads)[:, None] == src[None, :]).astype(BF)

        ins = resid = (x_loc, y)
        fresh, kv_all = [], []
        for layer in range(layers):
            first = layer == 0
            kvh, kv3, qh, dec, co, ci, do, di = front_call(dm, layer, first, ins, w_qkv, tab_c, tab_s, perm, lengths, ends, kc, vc)
            fresh.append(dec)

            def general(i, ctx):
                kv, q, edges, _ = lax.optimization_barrier((kvh, qh, ends, i))
                kvx = swap(kv, 'side', 2)
                kvs = (kv, swap(kv, 'side', 1), kvx, swap(kvx, 'side', 1))
                own, other = (general_attention(dm, jnp.concatenate([b[None], edges]), q, kvs) for b in (tp, 1 - tp))
                return own, swap(other, 'tp', 1)
            co, ci = lax.fori_loop(0, jnp.where(fast, 0, 1), general, (co, ci))
            o1, o2, p1, stat, kv3_x, kv3_p, kv3_q = post_call(dm, layer, first, resid, co, do, ci, di, kv3, w_out, w_gate, w_up, w_down)
            if layer == layers - 1:
                p2 = swap(o2, 'tp', 1)
            kv_all.append((kv3, kv3_p, kv3_x, kv3_q))
            ins, resid = (o1, o2, p1, stat), (o1, o2)
        k_prompt, v_prompt, k_new, v_new = tail_call(dm, inst_meta, lengths, kv_all, fresh, kc, vc)
        hidden, dec_out = close_call(dm, (o1, o2), (p1, p2))
        return hidden, dec_out[None], k_prompt, v_prompt, k_new, v_new

    return jax.shard_map(local_step, mesh=mesh,
                         in_specs=(rows_spec, P('pair'), P('pair'), P(), P(), P(), P(), P(), batch_spec, cache_spec, cache_spec, rows_spec),
                         out_specs=(rows_spec, batch_spec, prompt_spec, prompt_spec, cache_spec, cache_spec),
                         check_vma=False)
```

time: 6990 us -> 460 us (0.07)
  local copies, waits for them, and re-layouts: 2130 us -> 1.71 us
  matrix products: 1750 us -> 0 us
  blocking collectives: 1700 us -> 0 us
  other arithmetic: 1270 us -> 6.89 us
  Pallas kernels: 0 us -> 441 us
  waiting for transfers between devices: 70.3 us -> 0.01 us
    dot_general x34 -> x0, matrix products: 1750 us -> none  [the longest x4 281 us: finish_layer(): jnp.dot(activated, wd_l, preferred_element_type=jnp.float32)]
    psum x8 -> x0, blocking collectives: 1700 us -> none  [the longest x4 852 us: finish_layer(): lax.psum(jnp.dot(context, wo_l, preferred_element_type=jnp.float32), 'tp')]
    slice x18 -> x1, local copies, waits for them, and re-layouts: 1240 us -> 0.01 us  [local_step(): pos[:h]]
    scatter x257 -> x0, other arithmetic: 830 us -> none
    pallas_call x0 -> x6, Pallas kernels: none -> 441 us  [the longest x2 247 us: post_call(): pl.pallas_call(kern, out_shape=(part1, part2, part1, sds((m, LANES), F32)...]
    unnamed x81 -> x6, local copies, waits for them, and re-layouts: 323 us -> 0.9 us
    reduce_sum x13 -> x2, other arithmetic: 233 us -> 2.12 us  [the longest x1 1.34 us: local_step(): jnp.sum(jnp.where(mine, ends - req_len, 0))]
    squeeze x4 -> x0, local copies, waits for them, and re-layouts: 160 us -> none  [the longest x1 130 us: layer_weights(): qkv_l = w_qkv[layer]]
  transfers between devices with their start and end apart: 6 -> 1, of which waited for: 1 -> 0; matrix products, arithmetic and copies ran while one was open for 35% -> 0% of each run, Pallas kernels for 0% -> 8%
where the time goes in v1:
time: 460 us; the launch traced here: 451 us
  Pallas kernels  441 us (96%)
  other arithmetic  6.89 us (1%)
    pallas_call x2, Pallas kernels, post_call(): pl.pallas_call(kern, out_shape=(part1, part2, part1, sds((m, LANES), F32)...  247 us
    pallas_call x2, Pallas kernels, front_call(): pl.pallas_call(kern, out_shape=tuple((sds(s, BF) for s in outs)), in_spec...  155 us
    pallas_call x1, Pallas kernels, tail_call(): pl.pallas_call(kern, out_shape=(shape, shape, sds(kc.shape, BF), sds(vc.s...  34.4 us
  transfers between devices with their start and end apart: 1, of which 0 were waited for; matrix products, arithmetic and copies ran while one was open for 0% of the time, Pallas kernels for 8%

profile of v1, /device:TPU:0, one launch (start us, length us, event | category | flops | bytes accessed | tf_op | source)
XLA Modules:
  0.0 451.4 jit_solution(14277371597038205663)
XLA Ops:
  0.7 0.8 select_reduce_fusion.1.refs_7_.refs_9_
  1.4 0.1 select_reduce_fusion
  1.5 0.8 slice_bitcast_fusion.1
  2.4 0.8 fusion.refs_5_.refs_7_
  3.1 1.3 fusion.7
  5.1 0.1 add_convert_fusion
  5.2 1.0 fusion.1
  6.2 1.0 pad_maximum_fusion
  7.3 75.7 %front.2 = (bf16[2,16,512,128]{3,2,1,0:T(8,128)(2,1)}, bf16[2,512,16,128]{3,2,1,0:T(8,128)(2,1)}, bf16[16,512,128]{2,1,0:T(8,128)(2,1)S(1)}, bf16[3,32,16,128]{3...) custom-call(bf16[512,4096]{1,0:T(8,128)(2,1)} %refs_0_.3, ...), custom_call_target="tpu_custom_call" | custom-call | flops 27380416512 | bytes 50331648 | tf_op jit(solution)/shard_map/front/pallas_call | solution.py:416
  83.0 0.0 copy-start.7
  83.0 124.9 %post.2 = (bf16[272,2560]{1,0:T(8,128)(2,1)}, bf16[272,1536]{1,0:T(8,128)(2,1)}, bf16[272,2560]{1,0:T(8,128)(2,1)}, f32[272,128]{1,0:T(8,128)}, bf16[2,512,16,12...) custom-call(bf16[512,4096]{1,0:T(8,128)(2,1)} %refs_0_.3, ...), custom_call_target="tpu_custom_call" | custom-call | flops 82711674880 | bytes 168820736 | tf_op jit(solution)/shard_map/post/pallas_call | solution.py:731
  207.9 0.0 copy-done.7
  207.9 0.0 copy-start.8
  207.9 78.9 %front.3 = (bf16[2,16,512,128]{3,2,1,0:T(8,128)(2,1)}, bf16[2,512,16,128]{3,2,1,0:T(8,128)(2,1)}, bf16[16,512,128]{2,1,0:T(8,128)(2,1)S(1)}, bf16[3,32,16,128]{3...) custom-call(bf16[272,2560]{1,0:T(8,128)(2,1)} %get-tuple-element.212, ...), custom_call_target="tpu_custom_call" | custom-call | flops 27380416512 | bytes 50331648 | tf_op jit(solution)/shard_map/front/pallas_call | solution.py:416
  286.8 0.0 copy-done.8
  286.8 122.6 %post.3 = (bf16[272,2560]{1,0:T(8,128)(2,1)}, bf16[272,1536]{1,0:T(8,128)(2,1)}, bf16[272,2560]{1,0:T(8,128)(2,1)}, f32[272,128]{1,0:T(8,128)}, bf16[2,512,16,12...) custom-call(bf16[272,2560]{1,0:T(8,128)(2,1)} %get-tuple-element.212.refs_0_, ...), custom_call_target="tpu_custom_call" | custom-call | flops 82711674880 | bytes 168820736 | tf_op jit(solution)/shard_map/post/pallas_call | solution.py:731
  409.4 0.0 collective-permute-start.8
  409.5 1.8 pad_add_fusion.4.meta_ref
  411.2 34.4 %tail.1 = (bf16[1,2,896,16,128]{4,3,2,1,0:T(8,128)(2,1)}, bf16[1,2,896,16,128]{4,3,2,1,0:T(8,128)(2,1)}, bf16[1,2,32,64,16,128]{5,4,3,2,1,0:T(8,128)(2,1)}, bf16[1,2,32,64,16,128]{5,4,3,2,1,0:T(8,128)(2,1)}) custom-call(s32[2]{0:T(128)} %pad_add_fusion.4.meta_ref, s32[32]{0:T(128)} %bitcast.25, bf16[2,512,16,128]{3,2,1,0:T(8,128)(2,1)} %get-tuple-element.211.refs_6_.refs_0_, ...), custom_call_target="tpu_custom_call" | custom-call | flops 99999997952 | bytes 8388608 | tf_op jit(solution)/shard_map/tail/pallas_call | solution.py:820
  445.6 0.0 collective-permute-done.8.b2
  445.6 0.0 copy-start.6
  445.6 0.9 copy-done.6
  446.5 4.4 close.1
  (7 shorter events, 0.1 us)
Async XLA Ops:
  83.0 124.9 %copy-start.7 = (s32[4]{0:T(128)}, s32[4]{0:T(128)S(1)}, u32[]{:S(2)}) copy-start(s32[4]{0:T(128)S(1)} %get-tuple-element.494) | copy-start | bytes 52
  207.9 78.9 %copy-start.8 = (s32[4]{0:T(128)S(1)}, s32[4]{0:T(128)}, u32[]{:S(2)}) copy-start(s32[4]{0:T(128)} %copy-done.7) | copy-start | bytes 52
  409.4 36.2 %collective-permute-start.8 = (bf16[272,1536]{1,0:T(8,128)(2,1)}, bf16[272,1536]{1,0:T(8,128)(2,1)S(1)}, u32[]{:S(2)}, u32[]{:S(2)}) collective-permute-start(bf16[272,1536]{1,0:T(8,128)(2,1)} %get-tuple-element.226.a2), channel_id=1, source_target_pairs={{0,4},{4,0},{1,5},{5,1},{2,6},{6,2},{3,7},{7,3}} | collective-permute-start | bytes 2506760 | tf_op jit(solution)/shard_map/ppermute | solution.py:865
  445.6 0.9 copy-start.6

commit v2 on v1

--- a/solution.py
+++ b/solution.py
@@ -21,7 +21,8 @@
 HALVES = (0, WIDE)
 SUB = 16
 PER = 4
-EARLY_SENT = 5
+EARLY_SENT = (4, 3)
+NT = (((1,), (1,)), ((), ()))
 dma = pltpu.make_async_copy
 sds = jax.ShapeDtypeStruct
 sem = pltpu.SemaphoreType.DMA
@@ -64,13 +65,38 @@
         cp.wait()
 
 
-def norm_rows(src, dst, base, rows):
+def row_sum(x):
+    return jnp.sum(x, axis=1, keepdims=True)
+
+
+def row_max(x):
+    return jnp.max(x, axis=1, keepdims=True)
+
+
+def norm_rows(ref, base, rows):
+    group = 2 if rows % (2 * SUB) == 0 else 1
+
     def step(i):
-        sl = at(base + i * SUB, SUB, SUB)
-        wide = src[sl, :].astype(F32)
-        scale = lax.rsqrt(jnp.mean(wide * wide, axis=-1, keepdims=True) + NORM_EPS)
-        dst[sl, :] = (wide * scale).astype(BF)
-    each(rows // SUB, step)
+        for n in range(group):
+            sl = at(base + (group * i + n) * SUB, SUB, SUB)
+            wide = ref[sl, :].astype(F32)
+            scale = lax.rsqrt(jnp.mean(wide * wide, axis=-1, keepdims=True) + NORM_EPS)
+            ref[sl, :] = (wide * scale).astype(BF)
+    each(rows // SUB // group, step)
+
+
+def request_ends(len_ref):
+    ends = [len_ref[0]]
+    for r in range(1, 4):
+        ends.append(ends[-1] + len_ref[r])
+    return ends
+
+
+def segment_start(row, ends):
+    start = jnp.zeros_like(row)
+    for end in ends:
+        start = jnp.where(row >= end, end, start)
+    return start
 
 
 class Dims:
@@ -86,7 +112,7 @@
         self.lanes = (0, model, LANES)
 
 
-def front_call(dm, layer, first, ins, w_qkv, tab_c, tab_s, perm, lengths, ends, kc, vc):
+def front_call(dm, layer, first, ins, w_qkv, freq, lengths, req_len, kc, vc):
     nb = 4
     per_sec = dm.heads // PER
     steps = 3 * per_sec
@@ -98,14 +124,14 @@
     lead = dm.window - dm.rows
     batch, cache = kc.shape[2], kc.shape[3]
     flat = cache * dm.heads
-    ring = 3
+    ring = 4
     dsteps = batch // PER
     ni = len(ins)
 
     def kern(*refs):
         rin = refs[:ni]
-        (w_ref, c_ref, s_ref, perm_ref, len_ref, end_ref, k_ref, v_ref, kvh, kv3, qh, dec, co, ci, do, di,
-         xn, wb, kcat, qv, sd, dv, acc_a, acc_b, bias, sbuf, pbuf, cbuf, cr, dsc, dbuf, dout, o3, stat, raw,
+        (w_ref, f_ref, len_ref, req_ref, k_ref, v_ref, kvh, kv3, qh, dec, co, ci, do, di, tab_out,
+         tab, perm_ref, xn, wb, kcat, qv, sd, dv, acc_a, acc_b, bias, sbuf, pbuf, cbuf, cr, dsc, dbuf, dout, o3, stat,
          wsem, isem, csem, tsem, pss, prs, ess, ers, yss, yrs, lss, lrs) = refs[ni:]
         tp = lax.axis_index('tp')
         side = lax.axis_index('side')
@@ -123,34 +149,60 @@
                 out.append(dma(w_ref.at[layer, :, at(col, dm.hd)], wb.at[slot, :, pl.ds(n * dm.hd, dm.hd)], wsem.at[slot, n]))
             return out
 
+        def group_of(i):
+            return lax.rem(i + tp * (dsteps // 2), dsteps)
+
         def caches(i):
             slot = lax.rem(i, ring)
-            b = at(PER * i, PER, PER)
+            b = at(PER * group_of(i), PER, PER)
             return [dma(ref.at[0, layer, b], cr.at[slot, n], csem.at[slot, n]) for n, ref in enumerate((k_ref, v_ref))]
 
         if first:
             parts = [(rin[0], 0, 0, h), (rin[1], 0, h, d), (rin[0], h, k, h), (rin[1], d, k + h, d)]
             loads = [dma(ref.at[pl.ds(src, n)], xn.at[pl.ds(dst, n)], isem.at[i]) for i, (ref, src, dst, n) in enumerate(parts)]
         else:
-            own1, own2, peer1, ss_in = rin
+            own1, own2, peer1, ss_in, tab_in = rin
             cut = own1.shape[1]
             head_cols, tail_cols = pl.ds(0, cut), pl.ds(cut, dm.model - cut)
             top, low_rows = pl.ds(0, k), pl.ds(k, k)
             loads = [dma(own1, xn.at[top, head_cols], isem.at[0]), dma(own2, xn.at[top, tail_cols], isem.at[1]),
-                     dma(ss_in, stat.at[0], isem.at[2]), dma(peer1, xn.at[low_rows, head_cols], isem.at[3]), dma(own2, raw, tsem.at[0])]
+                     dma(ss_in, stat.at[0], isem.at[2]), dma(peer1, xn.at[low_rows, head_cols], isem.at[3]), dma(tab_in, tab, tsem.at[1])]
         begin(loads)
         for i in range(nb - 1):
             begin(wcopies(jnp.int32(i)))
-        begin(caches(jnp.int32(0)))
+        for i in range(2):
+            begin(caches(jnp.int32(i)))
 
         def zero(i):
             kcat[:, i, pl.ds(0, lead), :] = jnp.zeros((2, lead, dm.hd), BF)
         each(dm.heads, zero)
+        src = lax.broadcasted_iota(jnp.int32, perm_ref.shape, 0)
+        dst = lax.broadcasted_iota(jnp.int32, perm_ref.shape, 1)
+        perm_ref[...] = (lax.rem(src, dm.heads) * SUB + src // dm.heads == dst).astype(F32).astype(BF)
+        ends = request_ends(req_ref)
+
+        def table(row, pos):
+            size = pos.shape[0]
+            ang = pos.astype(F32) * f_ref[...]
+            sign = jnp.where(lax.broadcasted_iota(jnp.int32, pos.shape, 1) < dm.hd // 2, -1.0, 1.0)
+            tab[0, at(row, size, SUB), :] = jnp.cos(ang)
+            tab[1, at(row, size, SUB), :] = jnp.sin(ang) * sign
+
+        if first:
+            for b in range(2):
+                def rows_table(i):
+                    row = dm.rows * side + b * h + i * PER * SUB + lax.broadcasted_iota(jnp.int32, (PER * SUB, LANES), 0)
+                    table(b * k + i * PER * SUB, row - segment_start(row, ends))
+                each(h // SUB // PER, rows_table)
+                which = lax.broadcasted_iota(jnp.int32, (d, LANES), 0)
+                pos = jnp.zeros_like(which)
+                for i in range(d):
+                    pos = jnp.where(which == i, len_ref[b * d + i], pos)
+                table(b * k + h, pos)
         meet([{'side': lax.rem(side + i, 4)} for i in range(1, 4)] + [to_y])
         late = []
         if not first:
-            loads[4].wait()
-            late = [remote(raw, xn.at[low_rows, tail_cols], lss.at[0], lrs.at[0], to_y),
+            late = [remote(own2, xn.at[low_rows, tail_cols], lss.at[0], lrs.at[0], to_y),
                     remote(ss_in, stat.at[1], lss.at[1], lrs.at[1], to_y)]
             begin(late[::-1])
 
@@ -186,18 +238,28 @@
             pl.when(side == 1)(lambda: edge_copy(j, 2).wait_send())
             pl.when(side == 2)(lambda: edge_copy(j, 3).wait_send())
 
-        def dots(i, rows, acc):
+        def ahead(i):
             @pl.when(i + nb - 1 < npass * steps)
             def _():
                 begin(wcopies(i + nb - 1))
+
+        def fetch(i, more):
+            if more:
+                ahead(i)
             finish_all(wcopies(i))
+
+        def multiply(i, rows, acc):
             acc[...] = jnp.dot(xn[rows, :], wb[lax.rem(i, nb)], preferred_element_type=F32)
+
+        def dots(i, rows, acc):
+            fetch(i, True)
+            multiply(i, rows, acc)
 
         def epilogue(j, acc, blocks, is_q):
             sec, jj = j // per_sec, lax.rem(j, per_sec)
             for r0, b in blocks:
                 rows = slice(r0, r0 + k)
-                cv, sv = c_ref[at(b * k, k, SUB), :], s_ref[at(b * k, k, SUB), :]
+                cv, sv = tab[0, at(b * k, k, SUB), :], tab[1, at(b * k, k, SUB), :]
                 for n in range(PER):
                     head = PER * jj + n
                     val = acc[rows, n * dm.hd:(n + 1) * dm.hd].astype(BF).astype(F32)
@@ -222,11 +284,15 @@
             dots(jnp.int32(base), rows, acc_a)
 
             def pair(q):
-                dots(base + 2 * q + 1, rows, acc_b)
+                i = base + 2 * q + 1
+                fetch(i, True)
+                fetch(i + 1, False)
+                multiply(i, rows, acc_b)
                 epilogue(2 * q, acc_a, blocks, False)
+                multiply(i + 1, rows, acc_a)
+                epilogue(2 * q + 1, acc_b, blocks, False)
+                ahead(i + 1)
                 done(2 * q)
-                dots(base + 2 * q + 2, rows, acc_a)
-                epilogue(2 * q + 1, acc_b, blocks, False)
                 done(2 * q + 1)
             each(last // 2 - 1, pair)
             dots(jnp.int32(base + last - 1), rows, acc_b)
@@ -245,7 +311,7 @@
             epilogue(jnp.int32(steps - 1), acc, blocks, True)
 
         def apply_norm(n, base):
-            total_sq = jnp.sum(stat[n], axis=1, keepdims=True)
+            total_sq = row_sum(stat[n])
             stat[n] = jnp.broadcast_to(lax.rsqrt(total_sq / dm.model + NORM_EPS), (k, LANES))
 
             def step(i):
@@ -254,104 +320,108 @@
                     xn[sl, c:c + LANES] = (xn[sl, c:c + LANES].astype(F32) * stat[n, at(i * SUB, SUB, SUB), :]).astype(BF)
             each(k // SUB, step)
 
+        def cols(g):
+            return at(width * g, width)
+
+        def ctx_send(g):
+            return remote(cbuf.at[0, :, cols(g)], ci.at[:, cols(g)], yss.at[g], yrs.at[g], to_y)
+
+        dec_send = remote(dout.at[at((1 - tp) * d, d, SUB)], di, yss.at[per_sec], yrs.at[per_sec], to_y)
+        dec_keep = dma(dout.at[at(tp * d, d, SUB)], do, isem.at[0])
+
+        def score(b, w, head, n):
+            sbuf[n % 2, :, :w] = lax.dot_general(qv[head, b * h:(b + 1) * h, :], kcat[0, head, :w, :], NT, preferred_element_type=F32)
+
+        def value(ph, w, head, n):
+            s = sbuf[n % 2, :, :w] * (dm.hd ** -0.5 * LOG2E) + bias[:, :w]
+            p = jnp.exp2(s - row_max(s))
+            pbuf[n % 2, :, :w] = p.astype(BF)
+            tot = row_sum(p)
+            o = jnp.dot(pbuf[n % 2, :, :w], kcat[1, head, :w, :], preferred_element_type=F32)
+            cbuf[ph, :, at(head * dm.hd, dm.hd)] = (o / tot).astype(BF)
+
+        def turn_rows(rows, out):
+            x = jnp.concatenate([r.reshape(SUB * dm.heads, dm.hd) for r in rows], axis=1)
+            y = jnp.dot(perm_ref[...], x, preferred_element_type=F32).astype(BF)
+            for n, dst in enumerate(out):
+                dst(y[:, n * dm.hd:(n + 1) * dm.hd].reshape(SUB, dm.heads, dm.hd))
+
+        def decode_half(part):
+            col = lax.broadcasted_iota(jnp.int32, (dm.heads, flat), 1)
+            row = lax.broadcasted_iota(jnp.int32, (dm.heads, flat), 0)
+            pos = jnp.where(lax.rem(col, dm.heads) == row, col // dm.heads, flat)
+            scale = dm.hd ** -0.5
+            count = dsteps // 2
+
+            def look(n):
+                i = part * count + n
+
+                @pl.when(i + 2 < dsteps)
+                def _():
+                    begin(caches(i + 2))
+                finish_all(caches(i))
+                for r in range(PER):
+                    keys = cr[lax.rem(i, ring), 0, r].reshape(flat, dm.hd)
+                    dsc[n % 2, r] = lax.dot_general(dv[2, PER * group_of(i) + r], keys, NT, preferred_element_type=F32)
+
+            def gather(n):
+                i = part * count + n
+                for r in range(PER):
+                    bi = PER * group_of(i) + r
+                    q, kn, vn = (dv[c, bi].astype(F32) for c in (2, 0, 1))
+                    s = jnp.where(pos < len_ref[bi], dsc[n % 2, r] * scale, NEG)
+                    fresh = row_sum(q * kn) * scale
+                    top = jnp.maximum(row_max(s), fresh)
+                    p = jnp.exp(s - top)
+                    pf = jnp.exp(fresh - top)
+                    inv = 1.0 / (row_sum(p) + pf)
+                    vals = cr[lax.rem(i, ring), 1, r].reshape(flat, dm.hd)
+                    o = jnp.dot((p * inv).astype(BF), vals, preferred_element_type=F32)
+                    dbuf[bi] = o + (pf * inv).astype(BF).astype(F32) * vn
+
+            look(0)
+            for n in range(count):
+                if n + 1 < count:
+                    look(n + 1)
+                gather(n)
+
+        def put(ref, *idx):
+            def store(val):
+                ref[idx] = val
+            return store
+
+        def turn_block(b):
+            sl = at(b * d, d, SUB)
+            turn_rows([sd[n, :, sl, :] for n in range(3)], [put(dv, n, sl) for n in range(3)])
+
+            def block(i):
+                for n in range(PER):
+                    row = b * h + (PER * i + n) * SUB
+                    sl, own = at(row, SUB, SUB), at(lead + row, SUB, SUB)
+                    turn_rows([kcat[n2, :, own, :] for n2 in range(2)], [put(o3, n2, sl) for n2 in range(2)])
+            each(h // SUB // PER, block)
+
         if first:
-            finish_all(loads)
-            norm_rows(xn, xn, 0, m)
+            tab_copy = dma(tab, tab_out, tsem.at[1])
+            tab_copy.start()
+            for cp, (_, _, row, size) in zip(loads, parts):
+                cp.wait()
+                norm_rows(xn, row, size)
             blocks = [(0, 0), (k, 1)]
         else:
-            finish_all(loads[:3])
+            finish_all(loads[:3] + loads[4:])
             apply_norm(0, 0)
             run(0, [(0, tp)])
+            turn_block(tp)
+            decode_half(0)
             loads[3].wait()
             finish_all(late)
             apply_norm(1, k)
             blocks = [(0, 1 - tp)]
         run(npass - 1, blocks)
 
-        def cols(g):
-            return at(width * g, width)
-
-        def ctx_send(g):
-            return remote(cbuf.at[0, :, cols(g)], ci.at[:, cols(g)], yss.at[g], yrs.at[g], to_y)
-
-        dec_send = remote(dout.at[at((1 - tp) * d, d, SUB)], di, yss.at[per_sec], yrs.at[per_sec], to_y)
-        dec_keep = dma(dout.at[at(tp * d, d, SUB)], do, isem.at[0])
-
-        def score(b, w, head, n):
-            sbuf[n % 2, :, :w] = lax.dot_general(qv[head, b * h:(b + 1) * h, :], kcat[0, head, :w, :], (((1,), (1,)), ((), ())), preferred_element_type=F32)
-
-        def value(ph, w, head, n):
-            s = sbuf[n % 2, :, :w] * (dm.hd ** -0.5 * LOG2E) + bias[:, :w]
-            p = jnp.exp2(s - jnp.max(s, axis=1, keepdims=True))
-            pbuf[n % 2, :, :w] = p.astype(BF)
-            tot = jnp.sum(p, axis=1, keepdims=True)
-            o = jnp.dot(pbuf[n % 2, :, :w], kcat[1, head, :w, :], preferred_element_type=F32)
-            cbuf[ph, :, at(head * dm.hd, dm.hd)] = (o / tot).astype(BF)
-
-        def turn_rows(rows, out):
-            x = jnp.concatenate([r.reshape(SUB * dm.heads, dm.hd) for r in rows], axis=1)
-            y = jnp.dot(perm_ref[...], x, preferred_element_type=F32).astype(BF)
-            for n, dst in enumerate(out):
-                dst(y[:, n * dm.hd:(n + 1) * dm.hd].reshape(SUB, dm.heads, dm.hd))
-
-        def decode():
-            col = lax.broadcasted_iota(jnp.int32, (dm.heads, flat), 1)
-            row = lax.broadcasted_iota(jnp.int32, (dm.heads, flat), 0)
-            pos = jnp.where(lax.rem(col, dm.heads) == row, col // dm.heads, flat)
-            scale = dm.hd ** -0.5
-
-            def look(i, par):
-                @pl.when(i + 1 < dsteps)
-                def _():
-                    begin(caches(i + 1))
-                finish_all(caches(i))
-                for n in range(PER):
-                    keys = cr[lax.rem(i, ring), 0, n].reshape(flat, dm.hd)
-                    dsc[par, n] = lax.dot_general(dv[2, PER * i + n], keys, (((1,), (1,)), ((), ())), preferred_element_type=F32)
-
-            def gather(i, par):
-                for n in range(PER):
-                    bi = PER * i + n
-                    q, kn, vn = dv[2, bi].astype(F32), dv[0, bi].astype(F32), dv[1, bi].astype(F32)
-                    s = jnp.where(pos < len_ref[bi], dsc[par, n] * scale, NEG)
-                    fresh = jnp.sum(q * kn, axis=1, keepdims=True) * scale
-                    top = jnp.maximum(jnp.max(s, axis=1, keepdims=True), fresh)
-                    p = jnp.exp(s - top)
-                    pf = jnp.exp(fresh - top)
-                    inv = 1.0 / (jnp.sum(p, axis=1, keepdims=True) + pf)
-                    vals = cr[lax.rem(i, ring), 1, n].reshape(flat, dm.hd)
-                    o = jnp.dot((p * inv).astype(BF), vals, preferred_element_type=F32)
-                    dbuf[bi] = o + (pf * inv).astype(BF).astype(F32) * vn
-
-            look(jnp.int32(0), 0)
-
-            def two(t):
-                look(2 * t + 1, 1)
-                gather(2 * t, 0)
-                look(2 * t + 2, 0)
-                gather(2 * t + 1, 1)
-            each(dsteps // 2 - 1, two)
-            look(jnp.int32(dsteps - 1), 1)
-            gather(jnp.int32(dsteps - 2), 0)
-            gather(jnp.int32(dsteps - 1), 1)
-            for n in range(dm.heads):
-                dout[:, n * dm.hd:(n + 1) * dm.hd] = dbuf[:, n, :].astype(BF)
-
-        def put(ref, *idx):
-            def store(val):
-                ref[idx] = val
-            return store
-
-        def turn_all():
-            def block(i):
-                for n in range(PER):
-                    row = (PER * i + n) * SUB
-                    sl, own = at(row, SUB, SUB), at(lead + row, SUB, SUB)
-                    turn_rows([kcat[0, :, own, :], kcat[1, :, own, :]], [put(o3, 0, sl), put(o3, 1, sl)])
-            each(dm.rows // SUB // PER, block)
-
         kv3_copy = dma(o3, kv3, tsem.at[0])
-        kvh_copy = dma(kcat.at[:, :, pl.ds(lead, dm.rows)], kvh, tsem.at[1])
+        kvh_copy = dma(kcat.at[:, :, pl.ds(lead, dm.rows)], kvh, isem.at[2])
         q_copy = dma(qv, qh, tsem.at[2])
         dec_copy = dma(dv, dec, tsem.at[3])
 
@@ -369,23 +439,24 @@
 
             @pl.when(t == per_sec)
             def _():
-                for i in range(dm.dec // SUB):
-                    sl = pl.ds(i * SUB, SUB)
-                    turn_rows([sd[n, :, sl, :] for n in range(3)], [put(dv, n, sl) for n in range(3)])
-                turn_all()
+                ctx_send(per_sec - 1).start()
+                if first:
+                    each(2, turn_block)
+                    each(2, decode_half)
+                else:
+                    turn_block(1 - tp)
+                    decode_half(1)
+                for n in range(dm.heads):
+                    dout[:, n * dm.hd:(n + 1) * dm.hd] = dbuf[:, n, :].astype(BF)
                 begin([kv3_copy, kvh_copy, q_copy, dec_copy])
-                ctx_send(per_sec - 1).start()
-                decode()
 
             @pl.when(g == 0)
             def _():
-                row0 = dm.rows * side + h * b
+                rows = dm.rows * side + h * b + lax.broadcasted_iota(jnp.int32, (h, LANES), 0)
+                start = segment_start(rows, ends)
+                lane = dm.rows * side - lead + lax.broadcasted_iota(jnp.int32, (h, LANES), 1)
                 for c in range(dm.window // LANES):
-                    rows = row0 + lax.broadcasted_iota(jnp.int32, (h, LANES), 0)
-                    col = dm.rows * side - lead + c * LANES + lax.broadcasted_iota(jnp.int32, (h, LANES), 1)
-                    start = jnp.zeros_like(rows)
-                    for r in range(4):
-                        start = jnp.where(rows >= end_ref[r], end_ref[r], start)
+                    col = lane + c * LANES
                     bias[:, c * LANES:(c + 1) * LANES] = jnp.where((col >= start) & (col <= rows), 0.0, NEG)
             pl.when(t == per_sec)(lambda: begin([dec_send, dec_keep]))
 
@@ -400,6 +471,8 @@
             pl.when((ph == 0) & (g > 0))(lambda: ctx_send(g - 1).start())
         each(2 * per_sec, stage)
 
+        if first:
+            tab_copy.wait()
         keep = dma(cbuf.at[1], co, isem.at[1])
         keep.start()
         each(kv_steps, sent)
@@ -412,21 +485,23 @@
     flops = 2 * dm.all * dm.model * width * steps
     outs = [(2,) + heads, (2, dm.rows) + three, heads, (3, dm.dec) + three, (h, dm.loc), (h, dm.loc), (d, dm.loc), (d, dm.loc)]
     acc = pltpu.VMEM((m, width), F32)
+    tabs = sds((2, dm.all, LANES), F32)
     vec = sem((kv_steps,))
     return pl.pallas_call(
-        kern, out_shape=tuple(sds(s, BF) for s in outs),
-        in_specs=[ANY] * (ni + 1) + [WHOLE] * 3 + [SMEM] * 2 + [ANY] * 2, out_specs=(ANY,) * len(outs),
+        kern, out_shape=tuple(sds(s, BF) for s in outs) + (tabs,),
+        in_specs=[ANY] * (ni + 1) + [WHOLE] + [SMEM] * 2 + [ANY] * 2, out_specs=(ANY,) * (len(outs) + 1),
         scratch_shapes=[
+            pltpu.VMEM(tabs.shape, F32), pltpu.VMEM((SUB * dm.heads, SUB * dm.heads), BF),
             pltpu.VMEM((dm.all, dm.model), BF), pltpu.VMEM((nb, dm.model, width), BF), pltpu.VMEM((2, dm.heads, dm.window, dm.hd), BF),
             pltpu.VMEM(heads, BF), pltpu.VMEM((3, dm.heads, dm.dec, dm.hd), BF), pltpu.VMEM((3, dm.dec) + three, BF), acc, acc,
             pltpu.VMEM((h, dm.window), F32), pltpu.VMEM((2, h, dm.window), F32), pltpu.VMEM((2, h, dm.window), BF), pltpu.VMEM((2, h, dm.loc), BF),
             pltpu.VMEM((ring, 2, PER, cache) + three, BF), pltpu.VMEM((2, PER, dm.heads, flat), F32), pltpu.VMEM((batch,) + three, F32),
-            pltpu.VMEM((batch, dm.loc), BF), pltpu.VMEM((2, dm.rows) + three, BF), pltpu.VMEM((2, k, LANES), F32), pltpu.VMEM((k, dm.model - EARLY_SENT * CHUNK), BF),
+            pltpu.VMEM((batch, dm.loc), BF), pltpu.VMEM((2, dm.rows) + three, BF), pltpu.VMEM((2, k, LANES), F32),
             sem((nb, PER)), sem((4,)), sem((ring, 2)), sem((4,)), vec, vec, vec, vec,
             sem((per_sec + 1,)), sem((per_sec + 1,)), sem((2,)), sem((2,))],
         compiler_params=params(collective_id=layer, has_side_effects=True),
         cost_estimate=cost(flops, dm.model * width * steps * 2),
-        name="front")(*ins, w_qkv, tab_c, tab_s, perm, lengths, ends, kc, vc)
+        name="front")(*ins, w_qkv, freq, lengths, req_len, kc, vc)
 
 
 def general_attention(dm, meta, qh, kvs):
@@ -445,16 +520,11 @@
         kcat[:, :, :LANES, :] = jnp.zeros((2, PER, LANES, dm.hd), BF)
         begin(copies)
 
-        def seg_start(row):
-            st = jnp.zeros_like(row)
-            for r in range(4):
-                st = jnp.where(row >= meta_ref[1 + r], meta_ref[1 + r], st)
-            return st
-
-        n = (row0 + hb - seg_start(row0) // LANES * LANES + WIDE - 1) // WIDE
+        ends = [meta_ref[r] for r in range(1, meta_ref.shape[0])]
+        n = (row0 + hb - segment_start(row0, ends) // LANES * LANES + WIDE - 1) // WIDE
         begin_col = row0 + hb - WIDE * n
         rows = row0 + lax.broadcasted_iota(jnp.int32, (hb, WIDE), 0)
-        st_rows = seg_start(rows)
+        st_rows = segment_start(rows, ends)
         lanes = lax.broadcasted_iota(jnp.int32, (hb, WIDE), 1)
         mx[...] = jnp.full_like(mx, NEG)
         ls[...] = jnp.zeros_like(ls)
@@ -467,16 +537,16 @@
             bias[...] = jnp.where((col >= st_rows) & (col <= rows), 0.0, NEG)
             for i in range(PER):
                 keys = kcat[0, i, at(LANES + first, WIDE), :]
-                s = lax.dot_general(q_ref[i], keys, (((1,), (1,)), ((), ())), preferred_element_type=F32)
+                s = lax.dot_general(q_ref[i], keys, NT, preferred_element_type=F32)
                 s = s * (dm.hd ** -0.5 * LOG2E) + bias[...]
                 sc[i, :, at(c * WIDE, WIDE)] = s
-                mx[i] = jnp.maximum(mx[i], jnp.max(s, axis=1, keepdims=True))
+                mx[i] = jnp.maximum(mx[i], row_max(s))
         each(n, scores)
 
         def values(c):
             for i in range(PER):
                 p = jnp.exp2(sc[i, :, at(c * WIDE, WIDE)] - mx[i][:, :1])
-                ls[i] += jnp.sum(p, axis=1, keepdims=True)
+                ls[i] += row_sum(p)
                 vals = kcat[1, i, at(LANES + begin_col + WIDE * c, WIDE), :]
                 pv[i] += jnp.dot(p.astype(BF), vals, preferred_element_type=F32)
         each(n, values)
@@ -512,7 +582,8 @@
     h, d = dm.half, dm.dhalf
     crow = dm.rows // n_dn
     nr = len(resid)
-    cut = EARLY_SENT * CHUNK
+    early = EARLY_SENT[0 if first else -1]
+    cut = early * CHUNK
 
     def kern(*refs):
         rin = refs[:nr]
@@ -529,32 +600,28 @@
         def cols(j):
             return at(j * CHUNK, CHUNK)
 
-        def block(i, fn):
+        def out_block(i):
             slot = lax.rem(i, nb)
-
-            @pl.when(i < gu0)
+            return [dma(wo.at[layer, :, cols(i)], wb.at[slot], wsem.at[slot, 0])]
+
+        def gu_block(i, w=WIDE):
+            slot = lax.rem(i, nb)
+            c = at(core * ffh + (i - gu0) * WIDE, w)
+            return [dma(ref.at[layer, :, c], wb.at[slot, :, pl.ds(n * w, w)], wsem.at[slot, n]) for n, ref in enumerate((wg, wu))]
+
+        def dn_block(i, n):
+            slot = lax.rem(i, nb)
+            r = at(core * ffh + n * kc, ksz[n])
+            return [dma(wd.at[layer, r, cols((i - dn0) // nk)], wb.at[slot, pl.ds(0, ksz[n])], wsem.at[slot, 0])]
+
+        def start_late(i):
+            pl.when(i < dn0 - 1)(lambda: begin(gu_block(i)))
+
+            @pl.when(i >= dn0 - 1)
             def _():
-                fn(dma(wo.at[layer, :, cols(i)], wb.at[slot], wsem.at[slot, 0]))
-
-            for on, w in (((i >= gu0) & (i < dn0 - 1), WIDE), (i == dn0 - 1, rem)):
-                @pl.when(on)
-                def _(w=w):
-                    c = at(core * ffh + (i - gu0) * WIDE, w)
-                    for n, ref in enumerate((wg, wu)):
-                        fn(dma(ref.at[layer, :, c], wb.at[slot, :, pl.ds(n * w, w)], wsem.at[slot, n]))
-
-            j = i - dn0
-            for n in range(nk):
-                @pl.when((j >= 0) & (i < total) & (lax.rem(j, nk) == n))
-                def _(n=n):
-                    r = at(core * ffh + n * kc, ksz[n])
-                    fn(dma(wd.at[layer, r, cols(j // nk)], wb.at[slot, pl.ds(0, ksz[n])], wsem.at[slot, 0]))
-
-        def start(i):
-            block(i, lambda c: c.start())
-
-        def wait(i):
-            block(i, lambda c: c.wait())
+                pl.when(i == dn0 - 1)(lambda: begin(gu_block(i, rem)))
+                for n in range(nk):
+                    pl.when((i >= dn0) & (lax.rem(i - dn0, nk) == n))(lambda n=n: begin(dn_block(i, n)))
 
         mine, theirs = at(tp * h, h, SUB), at(tp * d, d, SUB)
         head_rows, tail_rows = pl.ds(0, h), pl.ds(h, d)
@@ -562,11 +629,12 @@
         if first:
             pairs += [(rin[0].at[mine], h1.at[head_rows]), (rin[1].at[theirs], h1.at[tail_rows])]
         else:
-            pairs += [(rin[0], h1.at[:, pl.ds(0, cut)]), (rin[1], h1.at[:, pl.ds(cut, dm.model - cut)])]
+            split = rin[0].shape[1]
+            pairs += [(rin[0], h1.at[:, pl.ds(0, split)]), (rin[1], h1.at[:, pl.ds(split, dm.model - split)])]
         loads = [dma(a, b, isem.at[n]) for n, (a, b) in enumerate(pairs)]
         begin(loads)
         for i in range(nb - 1):
-            start(jnp.int32(i))
+            begin(out_block(jnp.int32(i)))
         meet([to_core, to_x, to_y])
 
         def bulk(i):
@@ -597,8 +665,9 @@
 
         def out_step(i):
             pl.when(i > 0)(lambda: hsend(i - 1).start())
-            start(i + nb - 1)
-            wait(i)
+            pl.when(i + nb - 1 < gu0)(lambda: begin(out_block(i + nb - 1)))
+            pl.when(i + nb - 1 >= gu0)(lambda: begin(gu_block(i + nb - 1)))
+            finish_all(out_block(i))
             slot = lax.rem(i, nb)
             for n in HALVES:
                 acc = jnp.dot(xn[:m, :], wb[slot, :, n:n + WIDE], preferred_element_type=F32)
@@ -607,7 +676,7 @@
         each(n_out, out_step)
 
         def apply_norm(src, stat, base):
-            total_sq = jnp.sum(stat[...], axis=1, keepdims=True)
+            total_sq = row_sum(stat[...])
             stat[...] = jnp.broadcast_to(lax.rsqrt(total_sq / dm.model + NORM_EPS), stat.shape)
 
             def step(i):
@@ -625,9 +694,7 @@
         near.start()
         apply_norm(h1p, ssp, m)
 
-        def dots(i, acc):
-            start(i + nb - 1)
-            wait(i)
+        def multiply(i, acc):
             acc[...] = jnp.dot(xn[...], wb[lax.rem(i, nb)], preferred_element_type=F32)
 
         def glu(acc, j, w):
@@ -635,16 +702,22 @@
             upper = acc[:, w:2 * w].astype(BF).astype(F32)
             act[:, at(j * WIDE, w)] = (jax.nn.silu(gate) * upper).astype(BF)
 
-        dots(jnp.int32(gu0), acc_a)
+        begin(gu_block(jnp.int32(gu0 + nb - 1)))
+        finish_all(gu_block(jnp.int32(gu0)))
+        multiply(jnp.int32(gu0), acc_a)
 
         def gu_pair(q):
-            dots(gu0 + 2 * q + 1, acc_b)
+            i = gu0 + 2 * q + 1
+            start_late(i + nb - 1)
+            finish_all(gu_block(i) + gu_block(i + 1))
+            multiply(i, acc_b)
             glu(acc_a, 2 * q, WIDE)
-            dots(gu0 + 2 * q + 2, acc_a)
+            multiply(i + 1, acc_a)
             glu(acc_b, 2 * q + 1, WIDE)
+            start_late(i + nb)
         each(n_full // 2, gu_pair)
-        start(jnp.int32(dn0 - 1 + nb - 1))
-        wait(jnp.int32(dn0 - 1))
+        start_late(jnp.int32(dn0 - 2 + nb))
+        finish_all(gu_block(jnp.int32(dn0 - 1), rem))
         acc_b[:, :2 * rem] = jnp.dot(xn[...], wb[(dn0 - 1) % nb, :, :2 * rem], preferred_element_type=F32)
         glu(acc_a, n_full - 1, WIDE)
         glu(acc_b, n_full, rem)
@@ -653,17 +726,17 @@
             return remote(h1.at[:, cols(j)], ob.at[:, cols(j)], yss.at[j], yrs.at[j], to_y)
 
         def keeps(j, fn):
-            @pl.when(j < EARLY_SENT)
+            @pl.when(j < early)
             def _():
                 fn(dma(h1.at[:, cols(j)], oa.at[:, cols(j)], osem.at[j]))
 
-            @pl.when(j >= EARLY_SENT)
+            @pl.when(j >= early)
             def _():
-                fn(dma(h1.at[:, cols(j)], ot.at[:, cols(j - EARLY_SENT)], osem.at[j]))
+                fn(dma(h1.at[:, cols(j)], ot.at[:, cols(j - early)], osem.at[j]))
 
         def deliver(j):
             keeps(j, lambda c: c.start())
-            pl.when(j < EARLY_SENT)(lambda: share(j).start())
+            pl.when(j < early)(lambda: share(j).start())
 
         def psend_copy(j):
             return remote(psend.at[lax.rem(j, 2)], precv.at[j], pss.at[j], prs.at[j], to_core)
@@ -676,28 +749,29 @@
         def part(rows, slots, n):
             return sum(jnp.dot(act[rows, i * kc:i * kc + ksz[i]], wb[slots[i], :ksz[i], n:n + WIDE], preferred_element_type=F32) for i in range(nk))
 
-        def down(j, first):
+        def down(j, lead_in):
             i0 = dn0 + j * nk
-            if not first:
-                start(i0 + nb - 2)
-            start(i0 + nb - 1)
+            @pl.when(i0 + nb <= total)
+            def _():
+                if not lead_in:
+                    begin(dn_block(i0 + nb - 2, 0))
+                begin(dn_block(i0 + nb - 1, 1))
             slots = []
             for n in range(nk):
-                wait(i0 + n)
+                finish_all(dn_block(i0 + n, n))
                 slots.append(lax.rem(i0 + n, nb))
             half = lax.rem(j, 2)
             pl.when(j > 1)(lambda: psend_copy(j - 2).wait_send())
+            if not lead_in:
+                psend_copy(j - 1).wait_recv()
+                finish(j - 1)
             for n in HALVES:
                 psend[half, :, n:n + WIDE] = part(slice(m, 2 * m), slots, n)
-            if not first:
-                psend_copy(j - 1).wait_recv()
             psend_copy(j).start()
-            if not first:
-                finish(j - 1)
+            if not lead_in:
+                deliver(j - 1)
             for n in HALVES:
                 pown[half, :, n:n + WIDE] = part(slice(0, m), slots, n)
-            if not first:
-                deliver(j - 1)
             bulk(j).wait_recv()
             forward(j).start()
 
@@ -719,7 +793,7 @@
             bulk(j).wait_send()
             forward(j).wait()
             keeps(j, lambda c: c.wait())
-            pl.when(j < EARLY_SENT)(lambda: share(j).wait())
+            pl.when(j < early)(lambda: share(j).wait())
         each(n_dn, last)
 
     part1, part2 = sds((m, cut), BF), sds((m, dm.model - cut), BF)
@@ -737,11 +811,11 @@
             acc, acc, pair, pltpu.VMEM((n_dn, m, CHUNK), F32), pair, stat, stat,
             sem((nb, 2)), sem((6,)), vec, vec, vec, vec, vec, vec, vec, vec, vec, vec, vec, sem((2,)), sem((2,))],
         compiler_params=params(collective_id=2 + layer, has_side_effects=True),
-        cost_estimate=cost(2 * m * dm.model * (dm.model + 3 * dm.ff), dm.model * (2 * dm.model + 3 * dm.ff)),
+        cost_estimate=cost(PER * dm.all * dm.model * dm.ff, PER * dm.model * dm.ff),
         name="post")(*resid, co, do, ci, di, kv3, w_out, w_gate, w_up, w_down)
 
 
-def tail_call(dm, meta, lengths, kv3, news, kc, vc):
+def tail_call(dm, req_len, dest, lengths, kv3, news, kc, vc):
     layers, batch, cache = kc.shape[1:4]
     bits = [1 << b for b in reversed(range(dm.rows.bit_length()))]
     nsrc = len(kv3[0])
@@ -750,12 +824,16 @@
     ring = 6
     lag = 2
 
-    def kern(meta_ref, len_ref, *refs):
+    def kern(req_ref, dest_ref, len_ref, *refs):
         srcs, refs = refs[:layers * nsrc], refs[layers * nsrc:]
         dec, refs = refs[:layers], refs[layers:]
         kc_ref, vc_ref, ko, vo, kn, vn, buf, slots, dv, lsem, osem, dsem, isem, wsem = refs
         side = lax.axis_index('side')
-        start, length = meta_ref[0], meta_ref[1]
+        start, length = 0, 0
+        for r, end in enumerate(request_ends(req_ref)):
+            here = dest_ref[r] == side
+            start = jnp.where(here, end - req_ref[r], start)
+            length = jnp.where(here, req_ref[r], length)
 
         def pieces(fn):
             for k in range(nsrc):
@@ -819,12 +897,12 @@
     pair = sem((layers, 2))
     return pl.pallas_call(
         kern, out_shape=(shape, shape, sds(kc.shape, BF), sds(vc.shape, BF)),
-        in_specs=[SMEM, SMEM] + [ANY] * (len(flat) + layers + 2), out_specs=(ANY,) * 4,
+        in_specs=[SMEM] * 3 + [ANY] * (len(flat) + layers + 2), out_specs=(ANY,) * 4,
         scratch_shapes=[pltpu.VMEM((layers, 2, dm.max_req) + three, BF), pltpu.VMEM((ring, 2, PER, cache) + three, BF), pltpu.VMEM((layers,) + news[0].shape, BF),
                         sem((layers, nsrc, len(bits))), pair, sem((layers,)), sem((ring, 2)), sem((ring, 2))],
         compiler_params=params(),
         cost_estimate=cost(10**11, kc.size),
-        name="tail")(meta, lengths, *flat, *news, kc, vc)
+        name="tail")(req_len, dest, lengths, *flat, *news, kc, vc)
 
 
 def close_call(dm, mine, theirs):
@@ -833,22 +911,24 @@
 
     def kern(a1, a2, b1, b2, hid, dec, buf, lsem, osem):
         tp = lax.axis_index('tp')
-        loads = []
+        moves = []
         for n, (ref, blk, col) in enumerate(((a1, tp, 0), (a2, tp, cut), (b1, 1 - tp, 0), (b2, 1 - tp, cut))):
-            loads.append(dma(ref, buf.at[at(blk * k, k, SUB), pl.ds(col, ref.shape[1])], lsem.at[n]))
-        begin(loads)
-        finish_all(loads)
-        outs = []
-        for n in range(2):
-            outs.append(dma(buf.at[pl.ds(n * k, h)], hid.at[pl.ds(n * h, h)], osem.at[2 * n]))
-            outs.append(dma(buf.at[pl.ds(n * k + h, d)], dec.at[pl.ds(n * d, d)], osem.at[2 * n + 1]))
-        begin(outs)
-        finish_all(outs)
+            cs = pl.ds(col, ref.shape[1])
+            rows = blk * k
+            moves.append((dma(ref, buf.at[at(rows, k, SUB), cs], lsem.at[n]),
+                          [dma(buf.at[at(rows, h, SUB), cs], hid.at[at(blk * h, h, SUB), cs], osem.at[0, n]),
+                           dma(buf.at[at(rows + h, d, SUB), cs], dec.at[at(blk * d, d, SUB), cs], osem.at[1, n])]))
+        begin([load for load, _ in moves])
+        for load, outs in moves:
+            load.wait()
+            begin(outs)
+        for _, outs in moves:
+            finish_all(outs)
 
     return pl.pallas_call(
         kern, out_shape=(sds((dm.rows, dm.model), BF), sds((dm.dec, dm.model), BF)),
         in_specs=[ANY] * 4, out_specs=(ANY, ANY),
-        scratch_shapes=[pltpu.VMEM((dm.all, dm.model), BF), sem((4,)), sem((4,))],
+        scratch_shapes=[pltpu.VMEM((dm.all, dm.model), BF), sem((4,)), sem((2, 4))],
         compiler_params=params(), name="close")(*mine, *theirs)
 
 
@@ -872,34 +952,19 @@
         y = y_loc[0]
         lengths = clen_loc[0]
         dm = Dims(rows, y.shape[0], x_loc.shape[1], kc.shape[-2], kc.shape[-1], w_gate.shape[2], 2 * rows - rows // 4)
-        h, d = dm.half, dm.dhalf
 
         ends = jnp.sum(jnp.where(jnp.arange(side_size)[:, None] >= jnp.arange(side_size)[None, :], req_len[None, :], 0), axis=1)
-        row_ids = rows * side + jnp.arange(rows)
-        seg_start = jnp.max(jnp.where(row_ids[:, None] >= ends[None, :], ends[None, :], 0), axis=1)
-        pos = row_ids - seg_start
-        positions = jnp.concatenate([pos[:h], lengths[:d], pos[h:], lengths[d:]]).astype(F32)
+        mid = rows * side_size // 2
+        fast = mid - jnp.max(jnp.where(ends <= mid, ends, 0)) <= LANES
         half_dim = dm.hd // 2
         inv_freq = ROPE_BASE ** (-jnp.arange(half_dim, dtype=F32) / half_dim)
-        angles = positions[:, None] * inv_freq[None, :]
-        cos_val, sin_val = jnp.cos(angles), jnp.sin(angles)
-        tab_c = jnp.concatenate([cos_val, cos_val], axis=1)
-        tab_s = jnp.concatenate([-sin_val, sin_val], axis=1)
-
-        mine = dest == side
-        inst_meta = jnp.stack([jnp.sum(jnp.where(mine, ends - req_len, 0)), jnp.sum(jnp.where(mine, req_len, 0))])
-        mid = rows * side_size // 2
-        fast = mid - jnp.max(jnp.where(ends <= mid, ends, 0)) <= LANES
-
-        span = SUB * dm.heads
-        src = jnp.arange(span)
-        perm = ((src % dm.heads * SUB + src // dm.heads)[:, None] == src[None, :]).astype(BF)
+        freq = jnp.concatenate([inv_freq, inv_freq])[None]
 
         ins = resid = (x_loc, y)
         fresh, kv_all = [], []
         for layer in range(layers):
             first = layer == 0
-            kvh, kv3, qh, dec, co, ci, do, di = front_call(dm, layer, first, ins, w_qkv, tab_c, tab_s, perm, lengths, ends, kc, vc)
+            kvh, kv3, qh, dec, co, ci, do, di, tab = front_call(dm, layer, first, ins, w_qkv, freq, lengths, req_len, kc, vc)
             fresh.append(dec)
 
             def general(i, ctx):
@@ -913,8 +978,8 @@
             if layer == layers - 1:
                 p2 = swap(o2, 'tp', 1)
             kv_all.append((kv3, kv3_p, kv3_x, kv3_q))
-            ins, resid = (o1, o2, p1, stat), (o1, o2)
-        k_prompt, v_prompt, k_new, v_new = tail_call(dm, inst_meta, lengths, kv_all, fresh, kc, vc)
+            ins, resid = (o1, o2, p1, stat, tab), (o1, o2)
+        k_prompt, v_prompt, k_new, v_new = tail_call(dm, req_len, dest, lengths, kv_all, fresh, kc, vc)
         hidden, dec_out = close_call(dm, (o1, o2), (p1, p2))
         return hidden, dec_out[None], k_prompt, v_prompt, k_new, v_new
 

time: 460 us -> 419 us (0.911)
  Pallas kernels: 441 us -> 405 us
  other arithmetic: 6.89 us -> 2.03 us
    pallas_call x2, Pallas kernels: 247 us -> 219 us  [post_call(): pl.pallas_call(kern, out_shape=(part1, part2, part1, sds((m, LANES), F32)...]
    pallas_call x2, Pallas kernels: 155 us -> 149 us  [front_call(): pl.pallas_call(kern, out_shape=tuple((sds(s, BF) for s in outs)) + (tabs,...]
where the time goes in v2:
time: 419 us; the launch traced here: 412 us
  Pallas kernels  405 us (97%)
    pallas_call x2, Pallas kernels, post_call(): pl.pallas_call(kern, out_shape=(part1, part2, part1, sds((m, LANES), F32)...  219 us
    pallas_call x2, Pallas kernels, front_call(): pl.pallas_call(kern, out_shape=tuple((sds(s, BF) for s in outs)) + (tabs,...  149 us
    pallas_call x1, Pallas kernels, tail_call(): pl.pallas_call(kern, out_shape=(shape, shape, sds(kc.shape, BF), sds(vc.s...  32.6 us
  transfers between devices with their start and end apart: 1, of which 0 were waited for; matrix products, arithmetic and copies ran while one was open for 0% of the time, Pallas kernels for 8%

profile of v2, /device:TPU:0, one launch (start us, length us, event | category | flops | bytes accessed | tf_op | source)
XLA Modules:
  0.0 411.9 jit_solution(10837491656687014346)
XLA Ops:
  0.6 0.6 maximum_bitcast_fusion.refs_3_.refs_6_
  1.3 0.8 select_reduce_fusion
  2.0 0.6 fusion
  3.3 70.1 %front.2 = (bf16[2,16,512,128]{3,2,1,0:T(8,128)(2,1)}, bf16[2,512,16,128]{3,2,1,0:T(8,128)(2,1)}, bf16[16,512,128]{2,1,0:T(8,128)(2,1)S(1)}, bf16[3,32,16,128]{3...) custom-call(bf16[512,4096]{1,0:T(8,128)(2,1)} %refs_0_.3, ...), custom_call_target="tpu_custom_call" | custom-call | flops 27380416512 | bytes 50331648 | tf_op jit(solution)/shard_map/front/pallas_call | solution.py:490
  73.4 0.0 copy-start.7
  73.5 111.0 %post.2 = (bf16[272,2048]{1,0:T(8,128)(2,1)}, bf16[272,2048]{1,0:T(8,128)(2,1)}, bf16[272,2048]{1,0:T(8,128)(2,1)}, f32[272,128]{1,0:T(8,128)}, bf16[2,512,16,12...) custom-call(bf16[512,4096]{1,0:T(8,128)(2,1)} %refs_0_.3, ...), custom_call_target="tpu_custom_call" | custom-call | flops 98113159168 | bytes 180355072 | tf_op jit(solution)/shard_map/post/pallas_call | solution.py:805
  184.4 0.0 copy-done.7
  184.4 0.0 copy-start.8
  184.5 79.2 %front.3 = (bf16[2,16,512,128]{3,2,1,0:T(8,128)(2,1)}, bf16[2,512,16,128]{3,2,1,0:T(8,128)(2,1)}, bf16[16,512,128]{2,1,0:T(8,128)(2,1)S(1)}, bf16[3,32,16,128]{3...) custom-call(bf16[272,2048]{1,0:T(8,128)(2,1)} %get-tuple-element.213, ...), custom_call_target="tpu_custom_call" | custom-call | flops 27380416512 | bytes 50331648 | tf_op jit(solution)/shard_map/front/pallas_call | solution.py:490
  263.7 0.0 copy-done.8
  263.7 108.2 %post.3 = (bf16[272,1536]{1,0:T(8,128)(2,1)}, bf16[272,2560]{1,0:T(8,128)(2,1)}, bf16[272,1536]{1,0:T(8,128)(2,1)}, f32[272,128]{1,0:T(8,128)}, bf16[2,512,16,12...) custom-call(bf16[272,2048]{1,0:T(8,128)(2,1)} %get-tuple-element.213.refs_0_, ...), custom_call_target="tpu_custom_call" | custom-call | flops 98113159168 | bytes 180355072 | tf_op jit(solution)/shard_map/post/pallas_call | solution.py:805
  371.9 2.1 collective-permute-start.8
  374.0 32.6 %tail.1 = (bf16[1,2,896,16,128]{4,3,2,1,0:T(8,128)(2,1)}, bf16[1,2,896,16,128]{4,3,2,1,0:T(8,128)(2,1)}, bf16[1,2,32,64,16,128]{5,4,3,2,1,0:T(8,128)(2,1)}, bf16[1,2,32,64,16,128]{5,4,3,2,1,0:T(8,128)(2,1)}) custom-call(s32[4]{0:T(128)} %req_ref.1, s32[4]{0:T(128)} %dest_ref.1, s32[32]{0:T(128)} %bitcast.21, ...), custom_call_target="tpu_custom_call" | custom-call | flops 99999997952 | bytes 8388608 | tf_op jit(solution)/shard_map/tail/pallas_call | solution.py:898
  406.5 0.0 collective-permute-done.8.b2
  406.6 0.0 copy-start.6
  406.6 1.1 copy-done.6
  407.7 3.8 close.1
  (3 shorter events, 0.0 us)
Async XLA Ops:
  73.4 111.0 %copy-start.7 = (s32[4]{0:T(128)}, s32[4]{0:T(128)S(1)}, u32[]{:S(2)}) copy-start(s32[4]{0:T(128)S(1)} %get-tuple-element.484) | copy-start | bytes 52
  184.4 79.2 %copy-start.8 = (s32[4]{0:T(128)S(1)}, s32[4]{0:T(128)}, u32[]{:S(2)}) copy-start(s32[4]{0:T(128)} %copy-done.7) | copy-start | bytes 52
  371.9 34.7 %collective-permute-start.8 = (bf16[272,2560]{1,0:T(8,128)(2,1)}, bf16[272,2560]{1,0:T(8,128)(2,1)S(1)}, u32[]{:S(2)}, u32[]{:S(2)}) collective-permute-start(bf16[272,2560]{1,0:T(8,128)(2,1)} %get-tuple-element.228.a2), channel_id=1, source_target_pairs={{0,4},{4,0},{1,5},{5,1},{2,6},{6,2},{3,7},{7,3}} | collective-permute-start | bytes 4177928 | tf_op jit(solution)/shard_map/ppermute | solution.py:945
  406.6 1.1 copy-start.6

commit v3 on v2

--- a/solution.py
+++ b/solution.py
@@ -13,6 +13,7 @@
 ANY = pl.BlockSpec(memory_space=pl.ANY)
 SMEM = pl.BlockSpec(memory_space=pltpu.SMEM)
 WHOLE = pl.BlockSpec(memory_space=pltpu.VMEM)
+HBM = pl.BlockSpec(memory_space=pltpu.HBM)
 VMEM_LIMIT = 61 * 2**20
 LOG2E = 1.4426950408889634
 LANES = 128
@@ -132,7 +133,7 @@
         rin = refs[:ni]
         (w_ref, f_ref, len_ref, req_ref, k_ref, v_ref, kvh, kv3, qh, dec, co, ci, do, di, tab_out,
          tab, perm_ref, xn, wb, kcat, qv, sd, dv, acc_a, acc_b, bias, sbuf, pbuf, cbuf, cr, dsc, dbuf, dout, o3, stat,
-         wsem, isem, csem, tsem, pss, prs, ess, ers, yss, yrs, lss, lrs) = refs[ni:]
+         wsem, isem, csem, tsem, pss, prs, ess, ers, yss, yrs, lss, lrs, ksem) = refs[ni:]
         tp = lax.axis_index('tp')
         side = lax.axis_index('side')
         odd = lax.rem(side, 2)
@@ -168,10 +169,7 @@
             loads = [dma(own1, xn.at[top, head_cols], isem.at[0]), dma(own2, xn.at[top, tail_cols], isem.at[1]),
                      dma(ss_in, stat.at[0], isem.at[2]), dma(peer1, xn.at[low_rows, head_cols], isem.at[3]), dma(tab_in, tab, tsem.at[1])]
         begin(loads)
-        for i in range(nb - 1):
-            begin(wcopies(jnp.int32(i)))
-        for i in range(2):
-            begin(caches(jnp.int32(i)))
+        begin(wcopies(jnp.int32(0)))
 
         def zero(i):
             kcat[:, i, pl.ds(0, lead), :] = jnp.zeros((2, lead, dm.hd), BF)
@@ -320,11 +318,20 @@
                     xn[sl, c:c + LANES] = (xn[sl, c:c + LANES].astype(F32) * stat[n, at(i * SUB, SUB, SUB), :]).astype(BF)
             each(k // SUB, step)
 
+        def fill():
+            for i in range(1, nb - 1):
+                begin(wcopies(jnp.int32(i)))
+            for i in range(2):
+                begin(caches(jnp.int32(i)))
+
         def cols(g):
             return at(width * g, width)
 
         def ctx_send(g):
             return remote(cbuf.at[0, :, cols(g)], ci.at[:, cols(g)], yss.at[g], yrs.at[g], to_y)
+
+        def ctx_keep(g):
+            return dma(cbuf.at[1, :, cols(g)], co.at[:, cols(g)], ksem.at[g])
 
         dec_send = remote(dout.at[at((1 - tp) * d, d, SUB)], di, yss.at[per_sec], yrs.at[per_sec], to_y)
         dec_keep = dma(dout.at[at(tp * d, d, SUB)], do, isem.at[0])
@@ -406,10 +413,13 @@
             tab_copy.start()
             for cp, (_, _, row, size) in zip(loads, parts):
                 cp.wait()
+                if row == h:
+                    fill()
                 norm_rows(xn, row, size)
             blocks = [(0, 0), (k, 1)]
         else:
             finish_all(loads[:3] + loads[4:])
+            fill()
             apply_norm(0, 0)
             run(0, [(0, tp)])
             turn_block(tp)
@@ -469,16 +479,16 @@
                             score(bb, w, PER * g + n + 1, n + 1)
                         value(ph, w, PER * g + n, n)
             pl.when((ph == 0) & (g > 0))(lambda: ctx_send(g - 1).start())
+            pl.when((ph > 0) & (g > 0))(lambda: ctx_keep(g - 1).start())
         each(2 * per_sec, stage)
 
         if first:
             tab_copy.wait()
-        keep = dma(cbuf.at[1], co, isem.at[1])
-        keep.start()
+        ctx_keep(per_sec - 1).start()
         each(kv_steps, sent)
         finish_all([kv3_copy, kvh_copy, q_copy, dec_copy, dec_keep, dec_send])
+        each(per_sec, lambda g: ctx_keep(g).wait())
         each(per_sec, lambda g: ctx_send(g).wait())
-        keep.wait()
 
     heads = (dm.heads, dm.rows, dm.hd)
     three = (dm.heads, dm.hd)
@@ -498,7 +508,7 @@
             pltpu.VMEM((ring, 2, PER, cache) + three, BF), pltpu.VMEM((2, PER, dm.heads, flat), F32), pltpu.VMEM((batch,) + three, F32),
             pltpu.VMEM((batch, dm.loc), BF), pltpu.VMEM((2, dm.rows) + three, BF), pltpu.VMEM((2, k, LANES), F32),
             sem((nb, PER)), sem((4,)), sem((ring, 2)), sem((4,)), vec, vec, vec, vec,
-            sem((per_sec + 1,)), sem((per_sec + 1,)), sem((2,)), sem((2,))],
+            sem((per_sec + 1,)), sem((per_sec + 1,)), sem((2,)), sem((2,)), sem((per_sec,))],
         compiler_params=params(collective_id=layer, has_side_effects=True),
         cost_estimate=cost(flops, dm.model * width * steps * 2),
         name="front")(*ins, w_qkv, freq, lengths, req_len, kc, vc)
@@ -633,8 +643,7 @@
             pairs += [(rin[0], h1.at[:, pl.ds(0, split)]), (rin[1], h1.at[:, pl.ds(split, dm.model - split)])]
         loads = [dma(a, b, isem.at[n]) for n, (a, b) in enumerate(pairs)]
         begin(loads)
-        for i in range(nb - 1):
-            begin(out_block(jnp.int32(i)))
+        begin(out_block(jnp.int32(0)))
         meet([to_core, to_x, to_y])
 
         def bulk(i):
@@ -646,8 +655,10 @@
             return remote(kvx.at[:, r], kvq.at[:, r], fss.at[i], frs.at[i], to_core)
 
         near = remote(kv, kvp, dss.at[0], drs.at[0], to_core)
+        finish_all(loads)
+        for i in range(1, nb - 1):
+            begin(out_block(jnp.int32(i)))
         each(n_dn, lambda i: bulk(i).start())
-        finish_all(loads)
         for i in range(dm.heads):
             for n, t in enumerate((tp, 1 - tp)):
                 xn[:m, at((2 * i + t) * dm.hd, dm.hd)] = tmp[n, :, i * dm.hd:(i + 1) * dm.hd]
@@ -927,7 +938,7 @@
 
     return pl.pallas_call(
         kern, out_shape=(sds((dm.rows, dm.model), BF), sds((dm.dec, dm.model), BF)),
-        in_specs=[ANY] * 4, out_specs=(ANY, ANY),
+        in_specs=[HBM] * 4, out_specs=(ANY, ANY),
         scratch_shapes=[pltpu.VMEM((dm.all, dm.model), BF), sem((4,)), sem((2, 4))],
         compiler_params=params(), name="close")(*mine, *theirs)
 

time: 419 us -> 409 us (0.976)
  Pallas kernels: 405 us -> 394 us
    pallas_call x2, Pallas kernels: 219 us -> 210 us  [post_call(): pl.pallas_call(kern, out_shape=(part1, part2, part1, sds((m, LANES), F32)...]
where the time goes in v3:
time: 409 us; the launch traced here: 402 us
  Pallas kernels  394 us (96%)
    pallas_call x2, Pallas kernels, post_call(): pl.pallas_call(kern, out_shape=(part1, part2, part1, sds((m, LANES), F32)...  210 us
    pallas_call x2, Pallas kernels, front_call(): pl.pallas_call(kern, out_shape=tuple((sds(s, BF) for s in outs)) + (tabs,...  148 us
    pallas_call x1, Pallas kernels, tail_call(): pl.pallas_call(kern, out_shape=(shape, shape, sds(kc.shape, BF), sds(vc.s...  32.7 us
  transfers between devices with their start and end apart: 1, of which 0 were waited for; matrix products, arithmetic and copies ran while one was open for 0% of the time, Pallas kernels for 8%

profile of v3, /device:TPU:0, one launch (start us, length us, event | category | flops | bytes accessed | tf_op | source)
XLA Modules:
  0.0 401.9 jit_solution(5980545415353160899)
XLA Ops:
  0.6 0.6 maximum_bitcast_fusion.refs_3_.refs_6_
  1.3 0.8 select_reduce_fusion
  2.0 0.6 fusion
  3.3 70.0 %front.2 = (bf16[2,16,512,128]{3,2,1,0:T(8,128)(2,1)}, bf16[2,512,16,128]{3,2,1,0:T(8,128)(2,1)}, bf16[16,512,128]{2,1,0:T(8,128)(2,1)S(1)}, bf16[3,32,16,128]{3...) custom-call(bf16[512,4096]{1,0:T(8,128)(2,1)} %refs_0_.3, ...), custom_call_target="tpu_custom_call" | custom-call | flops 27380416512 | bytes 50331648 | tf_op jit(solution)/shard_map/front/pallas_call | solution.py:500
  73.3 0.0 copy-start.7
  73.3 104.8 %post.2 = (bf16[272,2048]{1,0:T(8,128)(2,1)}, bf16[272,2048]{1,0:T(8,128)(2,1)}, bf16[272,2048]{1,0:T(8,128)(2,1)}, f32[272,128]{1,0:T(8,128)}, bf16[2,512,16,12...) custom-call(bf16[512,4096]{1,0:T(8,128)(2,1)} %refs_0_.3, ...), custom_call_target="tpu_custom_call" | custom-call | flops 98113159168 | bytes 180355072 | tf_op jit(solution)/shard_map/post/pallas_call | solution.py:816
  178.1 0.0 copy-done.7
  178.1 0.0 copy-start.8
  178.1 78.3 %front.3 = (bf16[2,16,512,128]{3,2,1,0:T(8,128)(2,1)}, bf16[2,512,16,128]{3,2,1,0:T(8,128)(2,1)}, bf16[16,512,128]{2,1,0:T(8,128)(2,1)S(1)}, bf16[3,32,16,128]{3...) custom-call(bf16[272,2048]{1,0:T(8,128)(2,1)} %get-tuple-element.213, ...), custom_call_target="tpu_custom_call" | custom-call | flops 27380416512 | bytes 50331648 | tf_op jit(solution)/shard_map/front/pallas_call | solution.py:500
  256.4 0.0 copy-done.8
  256.5 104.9 %post.3 = (bf16[272,1536]{1,0:T(8,128)(2,1)}, bf16[272,2560]{1,0:T(8,128)(2,1)}, bf16[272,1536]{1,0:T(8,128)(2,1)}, f32[272,128]{1,0:T(8,128)}, bf16[2,512,16,12...) custom-call(bf16[272,2048]{1,0:T(8,128)(2,1)} %get-tuple-element.213.refs_0_, ...), custom_call_target="tpu_custom_call" | custom-call | flops 98113159168 | bytes 180355072 | tf_op jit(solution)/shard_map/post/pallas_call | solution.py:816
  361.3 2.5 collective-permute-start.8
  363.9 32.7 %tail.1 = (bf16[1,2,896,16,128]{4,3,2,1,0:T(8,128)(2,1)}, bf16[1,2,896,16,128]{4,3,2,1,0:T(8,128)(2,1)}, bf16[1,2,32,64,16,128]{5,4,3,2,1,0:T(8,128)(2,1)}, bf16[1,2,32,64,16,128]{5,4,3,2,1,0:T(8,128)(2,1)}) custom-call(s32[4]{0:T(128)} %req_ref.1, s32[4]{0:T(128)} %dest_ref.1, s32[32]{0:T(128)} %bitcast.21, ...), custom_call_target="tpu_custom_call" | custom-call | flops 99999997952 | bytes 8388608 | tf_op jit(solution)/shard_map/tail/pallas_call | solution.py:909
  396.6 0.0 collective-permute-done.8.b2
  396.6 0.0 copy-start.6
  396.6 1.1 copy-done.6
  397.7 3.8 close.1
  (3 shorter events, 0.0 us)
Async XLA Ops:
  73.3 104.8 %copy-start.7 = (s32[4]{0:T(128)}, s32[4]{0:T(128)S(1)}, u32[]{:S(2)}) copy-start(s32[4]{0:T(128)S(1)} %get-tuple-element.484) | copy-start | bytes 52
  178.1 78.3 %copy-start.8 = (s32[4]{0:T(128)S(1)}, s32[4]{0:T(128)}, u32[]{:S(2)}) copy-start(s32[4]{0:T(128)} %copy-done.7) | copy-start | bytes 52
  361.3 35.2 %collective-permute-start.8 = (bf16[272,2560]{1,0:T(8,128)(2,1)}, bf16[272,2560]{1,0:T(8,128)(2,1)S(1)}, u32[]{:S(2)}, u32[]{:S(2)}) collective-permute-start(bf16[272,2560]{1,0:T(8,128)(2,1)} %get-tuple-element.228.a2), channel_id=1, source_target_pairs={{0,4},{4,0},{1,5},{5,1},{2,6},{6,2},{3,7},{7,3}} | collective-permute-start | bytes 4177928 | tf_op jit(solution)/shard_map/ppermute | solution.py:956
  396.6 1.1 copy-start.6

commit v4 on v3

--- a/solution.py
+++ b/solution.py
@@ -1,5 +1,6 @@
 import jax
 import jax.numpy as jnp
+import numpy as np
 from jax import lax
 from jax.experimental import pallas as pl
 from jax.experimental.pallas import tpu as pltpu
@@ -655,7 +656,7 @@
             return remote(kvx.at[:, r], kvq.at[:, r], fss.at[i], frs.at[i], to_core)
 
         near = remote(kv, kvp, dss.at[0], drs.at[0], to_core)
-        finish_all(loads)
+        finish_all(loads[:PER])
         for i in range(1, nb - 1):
             begin(out_block(jnp.int32(i)))
         each(n_dn, lambda i: bulk(i).start())
@@ -663,6 +664,7 @@
             for n, t in enumerate((tp, 1 - tp)):
                 xn[:m, at((2 * i + t) * dm.hd, dm.hd)] = tmp[n, :, i * dm.hd:(i + 1) * dm.hd]
         ss[...] = jnp.zeros_like(ss)
+        finish_all(loads[PER:])
 
         def hsend(j):
             return remote(h1.at[:, cols(j)], h1p.at[:, cols(j)], hss.at[j], hrs.at[j], to_core)
@@ -968,8 +970,8 @@
         mid = rows * side_size // 2
         fast = mid - jnp.max(jnp.where(ends <= mid, ends, 0)) <= LANES
         half_dim = dm.hd // 2
-        inv_freq = ROPE_BASE ** (-jnp.arange(half_dim, dtype=F32) / half_dim)
-        freq = jnp.concatenate([inv_freq, inv_freq])[None]
+        inv_freq = np.float32(ROPE_BASE) ** (-np.arange(half_dim, dtype=np.float32) / half_dim)
+        freq = jnp.asarray(np.concatenate([inv_freq, inv_freq])[None], F32)
 
         ins = resid = (x_loc, y)
         fresh, kv_all = [], []

time: 409 us -> 407 us (level)
  no operation moved by 1% of the time
where the time goes in v4:
time: 407 us; the launch traced here: 400 us
  Pallas kernels  394 us (97%)
    pallas_call x2, Pallas kernels, post_call(): pl.pallas_call(kern, out_shape=(part1, part2, part1, sds((m, LANES), F32)...  209 us
    pallas_call x2, Pallas kernels, front_call(): pl.pallas_call(kern, out_shape=tuple((sds(s, BF) for s in outs)) + (tabs,...  148 us
    pallas_call x1, Pallas kernels, tail_call(): pl.pallas_call(kern, out_shape=(shape, shape, sds(kc.shape, BF), sds(vc.s...  32.4 us
  transfers between devices with their start and end apart: 1, of which 0 were waited for; matrix products, arithmetic and copies ran while one was open for 0% of the time, Pallas kernels for 8%

profile of v4, /device:TPU:0, one launch (start us, length us, event | category | flops | bytes accessed | tf_op | source)
XLA Modules:
  0.0 400.2 jit_solution(5535092230122106110)
XLA Ops:
  0.6 0.8 select_reduce_fusion
  1.4 0.6 fusion
  2.7 70.0 %front.2 = (bf16[2,16,512,128]{3,2,1,0:T(8,128)(2,1)}, bf16[2,512,16,128]{3,2,1,0:T(8,128)(2,1)}, bf16[16,512,128]{2,1,0:T(8,128)(2,1)S(1)}, bf16[3,32,16,128]{3...) custom-call(bf16[512,4096]{1,0:T(8,128)(2,1)} %refs_0_.3, ...), custom_call_target="tpu_custom_call" | custom-call | flops 27380416512 | bytes 50331648 | tf_op jit(solution)/shard_map/front/pallas_call | solution.py:501
  72.7 0.0 copy-start.7
  72.7 104.8 %post.2 = (bf16[272,2048]{1,0:T(8,128)(2,1)}, bf16[272,2048]{1,0:T(8,128)(2,1)}, bf16[272,2048]{1,0:T(8,128)(2,1)}, f32[272,128]{1,0:T(8,128)}, bf16[2,512,16,12...) custom-call(bf16[512,4096]{1,0:T(8,128)(2,1)} %refs_0_.3, ...), custom_call_target="tpu_custom_call" | custom-call | flops 98113159168 | bytes 180355072 | tf_op jit(solution)/shard_map/post/pallas_call | solution.py:818
  177.5 0.0 copy-done.7
  177.5 0.0 copy-start.8
  177.5 78.3 %front.3 = (bf16[2,16,512,128]{3,2,1,0:T(8,128)(2,1)}, bf16[2,512,16,128]{3,2,1,0:T(8,128)(2,1)}, bf16[16,512,128]{2,1,0:T(8,128)(2,1)S(1)}, bf16[3,32,16,128]{3...) custom-call(bf16[272,2048]{1,0:T(8,128)(2,1)} %get-tuple-element.213, ...), custom_call_target="tpu_custom_call" | custom-call | flops 27380416512 | bytes 50331648 | tf_op jit(solution)/shard_map/front/pallas_call | solution.py:501
  255.8 0.0 copy-done.8
  255.8 104.3 %post.3 = (bf16[272,1536]{1,0:T(8,128)(2,1)}, bf16[272,2560]{1,0:T(8,128)(2,1)}, bf16[272,1536]{1,0:T(8,128)(2,1)}, f32[272,128]{1,0:T(8,128)}, bf16[2,512,16,12...) custom-call(bf16[272,2048]{1,0:T(8,128)(2,1)} %get-tuple-element.213.refs_0_, ...), custom_call_target="tpu_custom_call" | custom-call | flops 98113159168 | bytes 180355072 | tf_op jit(solution)/shard_map/post/pallas_call | solution.py:818
  360.1 2.3 collective-permute-start.8
  362.4 32.4 %tail.1 = (bf16[1,2,896,16,128]{4,3,2,1,0:T(8,128)(2,1)}, bf16[1,2,896,16,128]{4,3,2,1,0:T(8,128)(2,1)}, bf16[1,2,32,64,16,128]{5,4,3,2,1,0:T(8,128)(2,1)}, bf16[1,2,32,64,16,128]{5,4,3,2,1,0:T(8,128)(2,1)}) custom-call(s32[4]{0:T(128)} %req_ref.1, s32[4]{0:T(128)} %dest_ref.1, s32[32]{0:T(128)} %bitcast.19, ...), custom_call_target="tpu_custom_call" | custom-call | flops 99999997952 | bytes 8388608 | tf_op jit(solution)/shard_map/tail/pallas_call | solution.py:911
  394.8 0.0 collective-permute-done.8.b2
  394.8 0.0 copy-start.6
  394.8 1.1 copy-done.6
  395.9 3.8 close.1
  (2 shorter events, 0.0 us)
Async XLA Ops:
  72.7 104.8 %copy-start.7 = (s32[4]{0:T(128)}, s32[4]{0:T(128)S(1)}, u32[]{:S(2)}) copy-start(s32[4]{0:T(128)S(1)} %get-tuple-element.484) | copy-start | bytes 52
  177.5 78.3 %copy-start.8 = (s32[4]{0:T(128)S(1)}, s32[4]{0:T(128)}, u32[]{:S(2)}) copy-start(s32[4]{0:T(128)} %copy-done.7) | copy-start | bytes 52
  360.1 34.7 %collective-permute-start.8 = (bf16[272,2560]{1,0:T(8,128)(2,1)}, bf16[272,2560]{1,0:T(8,128)(2,1)S(1)}, u32[]{:S(2)}, u32[]{:S(2)}) collective-permute-start(bf16[272,2560]{1,0:T(8,128)(2,1)} %get-tuple-element.228.a2), channel_id=1, source_target_pairs={{0,4},{4,0},{1,5},{5,1},{2,6},{6,2},{3,7},{7,3}} | collective-permute-start | bytes 4177928 | tf_op jit(solution)/shard_map/ppermute | solution.py:958
  394.8 1.1 copy-start.6
